TPU v7x, 32 devices: a whole 2x2x4 slice. The times are simulated.
32 devices in a mesh: batch: 4 (over y, x), seq: 8 (over z, core).
Axes of the slice: x: 2, y: 2, z: 4, core: 2. Of those that a mesh axis runs over, the one named last changes fastest.
Arguments:
- inputs: bfloat16 [16, 3072, 512], P('batch', 'seq'), may hold values from -6 to 6
- cotangent: bfloat16 [16, 3072, 512], P('batch', 'seq'), may hold values from -6 to 6
- doc_lengths: int32 [16, 8], P('batch'), may hold values from 1 to 1536, 3072 in all within a row
- pool_weight: bfloat16 [1536, 512], replicated, may hold values from -0.15625 to 0.15625
- pool_bias: float32 [512], replicated, may hold values from -3 to 3
- gain_one: float32 [512], replicated, may hold values from 0.25 to 1.75
- shift_one: float32 [512], replicated, may hold values from -1.75 to 1.75
- query_weight: bfloat16 [512, 512], replicated, may hold values from -0.375 to 0.375
- key_weight: bfloat16 [512, 512], replicated, may hold values from -0.375 to 0.375
- value_weight: bfloat16 [512, 512], replicated, may hold values from -0.25 to 0.25
- out_weight: bfloat16 [512, 512], replicated, may hold values from -0.75 to 0.75
- slopes: float32 [8], replicated, may hold values from 0.0003 to 0.1
- gain_two: float32 [512], replicated, may hold values from 0.25 to 1.75
- shift_two: float32 [512], replicated, may hold values from -1.75 to 1.75
- inner_weight: bfloat16 [512, 2048], replicated, may hold values from -0.25 to 0.25
- inner_bias: float32 [2048], replicated, may hold values from -3 to 3
- outer_weight: bfloat16 [2048, 512], replicated, may hold values from -0.125 to 0.125
- outer_bias: float32 [512], replicated, may hold values from -3 to 3
- up_weight: bfloat16 [512, 1536], replicated, may hold values from -0.25 to 0.25
- up_bias: float32 [1536], replicated, may hold values from -3 to 3
Outputs:
- output: bfloat16 [16, 3072, 512], P('batch', 'seq')
- input_grad: float32 [16, 3072, 512], P('batch', 'seq')
- grad_pool_weight: float32 [1536, 512], replicated
- grad_pool_bias: float32 [512], replicated
- grad_gain_one: float32 [512], replicated
- grad_shift_one: float32 [512], replicated
- grad_query_weight: float32 [512, 512], replicated
- grad_key_weight: float32 [512, 512], replicated
- grad_value_weight: float32 [512, 512], replicated
- grad_out_weight: float32 [512, 512], replicated
- grad_slopes: float32 [8], replicated
- grad_gain_two: float32 [512], replicated
- grad_shift_two: float32 [512], replicated
- grad_inner_weight: float32 [512, 2048], replicated
- grad_inner_bias: float32 [2048], replicated
- grad_outer_weight: float32 [2048, 512], replicated
- grad_outer_bias: float32 [512], replicated
- grad_up_weight: float32 [512, 1536], replicated
- grad_up_bias: float32 [1536], replicated
Inputs may be any that keep to these rules, and one draw needn't show every extreme that they name: `doc_lengths`: the 8 document lengths of each row sum to 3072.
All inputs are finite; a program needn't handle non-finite values.
Results may differ from a plain program's by a relative error of at most 0.015.
Values may be sent and summed in bfloat16 or wider, within the bound.
A program may use at most 256 MiB of HBM per device.

v0:
```python
import jax
import jax.numpy as jnp
from jax import lax
from jax.sharding import PartitionSpec as P

norm_eps = 1e-05


def shifted_2(block, axis, distance):
    devices = range(lax.axis_size(axis))
    route = [(i - distance, i) for i in devices if i - distance in devices]
    return lax.ppermute(block, axis, route)


def matmul(left, right):
    return jnp.dot(left, right, preferred_element_type=jnp.float32)


def norm_rows(values_in, norm_gain, norm_shift):
    centre = values_in - jnp.mean(values_in, axis=-1, keepdims=True)
    spread = jnp.mean(centre * centre, axis=-1, keepdims=True)
    return centre * lax.rsqrt(spread + norm_eps) * norm_gain + norm_shift


def exact_gelu(values_in):
    return jax.nn.gelu(values_in, approximate=False)


def masked_scores(query_heads, key_heads, slopes, distance, allowed, score_scale):
    raw_scores = jnp.einsum(
        "rqhd,rkhd->rhqk", query_heads, key_heads, preferred_element_type=jnp.float32
    )
    raw_scores = raw_scores * score_scale - slopes[None, :, None, None] * distance[None, None]
    return jnp.where(allowed[:, None], raw_scores, -1e30)


def local(
    inputs,
    cotangent,
    doc_lengths,
    pool_weight,
    pool_bias,
    gain_one,
    shift_one,
    query_weight,
    key_weight,
    value_weight,
    out_weight,
    slopes,
    gain_two,
    shift_two,
    inner_weight,
    inner_bias,
    outer_weight,
    outer_bias,
    up_weight,
    up_bias,
):
    row_count, block_len, feature_width = inputs.shape
    short_len = block_len // 3
    head_count = slopes.shape[0]
    head_dim = feature_width // head_count
    score_scale = head_dim ** (-0.5)
    total_short = short_len * lax.axis_size("seq")
    offset = lax.axis_index("seq") * short_len
    token_count = row_count * short_len
    left_rim = shifted_2(inputs[:, block_len - 2 :, :], "seq", 1)
    shifted = jnp.concatenate([left_rim, inputs[:, : block_len - 2, :]], axis=1)
    groups = shifted.reshape(token_count, 3 * feature_width)
    pooled = matmul(groups, pool_weight) + pool_bias
    normed_one = norm_rows(pooled, gain_one, shift_one).astype(jnp.bfloat16)
    query = matmul(normed_one, query_weight).astype(jnp.bfloat16)
    key_rows = matmul(normed_one, key_weight).astype(jnp.bfloat16)
    value_rows = matmul(normed_one, value_weight).astype(jnp.bfloat16)
    doc_ends = jnp.cumsum(doc_lengths, axis=1)
    key_places = jnp.arange(total_short, dtype=jnp.int32)
    key_docs = jnp.sum(
        (doc_ends[:, None, :] <= 3 * key_places[None, :, None]).astype(jnp.int32), axis=2
    )
    query_docs = lax.dynamic_slice_in_dim(key_docs, offset, short_len, 1)
    query_places = offset + jnp.arange(short_len, dtype=jnp.int32)
    distance = (query_places[:, None] - key_places[None, :]).astype(jnp.float32)
    allowed = (distance >= 0.0)[None] & (query_docs[:, :, None] == key_docs[:, None, :])
    key_block = key_rows.reshape(row_count, short_len, feature_width)
    value_block = value_rows.reshape(row_count, short_len, feature_width)
    all_keys, all_values = (
        lax.all_gather(key_block, "seq", axis=1, tiled=True),
        lax.all_gather(value_block, "seq", axis=1, tiled=True),
    )
    query_heads = query.reshape(row_count, short_len, head_count, head_dim)
    key_heads = all_keys.reshape(row_count, total_short, head_count, head_dim)
    value_heads = all_values.reshape(row_count, total_short, head_count, head_dim)
    scores = masked_scores(query_heads, key_heads, slopes, distance, allowed, score_scale)
    row_top = jnp.max(scores, axis=-1, keepdims=True)
    exponent = jnp.exp(scores - row_top)
    row_total = jnp.sum(exponent, axis=-1, keepdims=True)
    log_total = row_top + jnp.log(row_total)
    probs_low = (exponent / row_total).astype(jnp.bfloat16)
    attended = jnp.einsum(
        "rhqk,rkhd->rqhd", probs_low, value_heads, preferred_element_type=jnp.float32
    )
    attended = attended.reshape(token_count, feature_width).astype(jnp.bfloat16)
    residual_one = pooled + matmul(attended, out_weight)
    normed_two = norm_rows(residual_one, gain_two, shift_two).astype(jnp.bfloat16)
    inner_sum = matmul(normed_two, inner_weight) + inner_bias
    activated = exact_gelu(inner_sum).astype(jnp.bfloat16)
    residual_two = residual_one + matmul(activated, outer_weight) + outer_bias
    residual_low = residual_two.astype(jnp.bfloat16)
    raised = matmul(residual_low, up_weight) + up_bias
    output = (
        inputs.astype(jnp.float32) + raised.reshape(row_count, block_len, feature_width)
    ).astype(jnp.bfloat16)
    grad_raised = cotangent.reshape(token_count, 3 * feature_width)
    grad_up_weight = matmul(residual_low.T, grad_raised)
    grad_up_bias = jnp.sum(grad_raised.astype(jnp.float32), axis=0)
    grad_resid = matmul(grad_raised, up_weight.T)
    grad_branch = grad_resid.astype(jnp.bfloat16)
    grad_outer_weight = matmul(activated.T, grad_branch)
    grad_outer_bias = jnp.sum(grad_branch.astype(jnp.float32), axis=0)
    grad_active = matmul(grad_branch, outer_weight.T)
    unused_gelu, gelu_back = jax.vjp(exact_gelu, inner_sum)
    grad_inner = gelu_back(grad_active)[0].astype(jnp.bfloat16)
    grad_inner_weight = matmul(normed_two.T, grad_inner)
    grad_inner_bias = jnp.sum(grad_inner.astype(jnp.float32), axis=0)
    grad_normed_two = matmul(grad_inner, inner_weight.T)
    unused_two, norm_back_two = jax.vjp(norm_rows, residual_one, gain_two, shift_two)
    grad_mix_part, grad_gain_two, grad_shift_two = norm_back_two(grad_normed_two)
    grad_mixed = grad_resid + grad_mix_part
    grad_attn = grad_mixed.astype(jnp.bfloat16)
    grad_out_weight = matmul(attended.T, grad_attn)
    grad_attended = matmul(grad_attn, out_weight.T).astype(jnp.bfloat16)
    back_keys, back_values = (all_keys, all_values)
    key_heads = back_keys.reshape(row_count, total_short, head_count, head_dim)
    value_heads = back_values.reshape(row_count, total_short, head_count, head_dim)
    scores = masked_scores(query_heads, key_heads, slopes, distance, allowed, score_scale)
    probs = jnp.exp(scores - log_total)
    grad_heads = grad_attended.reshape(row_count, short_len, head_count, head_dim)
    grad_probs = jnp.einsum(
        "rqhd,rkhd->rhqk", grad_heads, value_heads, preferred_element_type=jnp.float32
    )
    row_term = jnp.sum(probs * grad_probs, axis=-1, keepdims=True)
    grad_scores = (probs * (grad_probs - row_term)).astype(jnp.bfloat16)
    grad_slopes = -jnp.sum(grad_scores.astype(jnp.float32) * distance[None, None], axis=(0, 2, 3))
    grad_query = jnp.einsum(
        "rhqk,rkhd->rqhd", grad_scores, key_heads, preferred_element_type=jnp.float32
    )
    grad_query = (grad_query * score_scale).reshape(token_count, feature_width).astype(jnp.bfloat16)
    grad_value_term = jnp.einsum(
        "rhqk,rqhd->rkhd",
        probs.astype(jnp.bfloat16),
        grad_heads,
        preferred_element_type=jnp.float32,
    ).reshape(row_count, total_short, feature_width)
    grad_key_term = jnp.einsum(
        "rhqk,rqhd->rkhd", grad_scores, query_heads, preferred_element_type=jnp.float32
    )
    grad_key_term = (grad_key_term * score_scale).reshape(row_count, total_short, feature_width)
    grad_keys, grad_values = (
        lax.psum_scatter(
            grad_key_term.astype(jnp.bfloat16), "seq", scatter_dimension=1, tiled=True
        ).astype(jnp.float32),
        lax.psum_scatter(
            grad_value_term.astype(jnp.bfloat16), "seq", scatter_dimension=1, tiled=True
        ).astype(jnp.float32),
    )
    grad_keys = grad_keys.reshape(token_count, feature_width).astype(jnp.bfloat16)
    grad_values = grad_values.reshape(token_count, feature_width).astype(jnp.bfloat16)
    grad_query_weight = matmul(normed_one.T, grad_query)
    grad_key_weight = matmul(normed_one.T, grad_keys)
    grad_value_weight = matmul(normed_one.T, grad_values)
    grad_normed_one = matmul(grad_query, query_weight.T) + matmul(grad_keys, key_weight.T)
    grad_normed_one = grad_normed_one + matmul(grad_values, value_weight.T)
    unused_one, norm_back_one = jax.vjp(norm_rows, pooled, gain_one, shift_one)
    grad_pool_part, grad_gain_one, grad_shift_one = norm_back_one(grad_normed_one)
    grad_pooled = (grad_mixed + grad_pool_part).astype(jnp.bfloat16)
    grad_pool_weight = matmul(groups.T, grad_pooled)
    grad_pool_bias = jnp.sum(grad_pooled.astype(jnp.float32), axis=0)
    grad_groups = matmul(grad_pooled, pool_weight.T).reshape(row_count, block_len, feature_width)
    back_rim = shifted_2(grad_groups[:, :2, :], "seq", -1)
    input_grad = cotangent.astype(jnp.float32) + jnp.concatenate(
        [grad_groups[:, 2:, :], back_rim], axis=1
    )
    local_grads = (
        grad_pool_weight,
        grad_pool_bias,
        grad_gain_one,
        grad_shift_one,
        grad_query_weight,
        grad_key_weight,
        grad_value_weight,
        grad_out_weight,
        grad_slopes,
        grad_gain_two,
        grad_shift_two,
        grad_inner_weight,
        grad_inner_bias,
        grad_outer_weight,
        grad_outer_bias,
        grad_up_weight,
        grad_up_bias,
    )
    summed = lax.psum(
        (
            local_grads[0],
            local_grads[1],
            local_grads[2],
            local_grads[3],
            local_grads[4],
            local_grads[5],
            local_grads[6],
            local_grads[7],
            local_grads[8],
            local_grads[9],
            local_grads[10],
            local_grads[11],
            local_grads[12],
            local_grads[13],
            local_grads[14],
            local_grads[15],
            local_grads[16],
        ),
        ("batch", "seq"),
    )
    return (output, input_grad) + tuple(summed)


def solution(mesh):
    in_specs = (
        P("batch", "seq", None),
        P("batch", "seq", None),
        P("batch", None),
        P(),
        P(),
        P(),
        P(),
        P(),
        P(),
        P(),
        P(),
        P(),
        P(),
        P(),
        P(),
        P(),
        P(),
        P(),
        P(),
        P(),
    )
    out_specs = (
        P("batch", "seq", None),
        P("batch", "seq", None),
        P(),
        P(),
        P(),
        P(),
        P(),
        P(),
        P(),
        P(),
        P(),
        P(),
        P(),
        P(),
        P(),
        P(),
        P(),
        P(),
        P(),
    )
    return jax.shard_map(local, mesh=mesh, in_specs=in_specs, out_specs=out_specs, check_vma=False)
```

profile of v0, /device:TPU:0, one launch (start us, length us, event | category | flops | bytes accessed | tf_op | source)
XLA Modules:
  0.0 645.3 jit_solution(3817851279037618391)
XLA Ops:
  29.3 4.4 convert_reduce_fusion.2
  46.1 29.2 %all-gather.5.cloned.1.call-done = bf16[4,1024,512]{2,1,0:T(8,128)(2,1)} async-done(((bf16[4,128,512]{2,1,0:T(8,128)(2,1)}), bf16[4,1024,512]{2,1,0:T(8,128)(2,1)}) %all-gather.5.cloned.1.call-update) | async-done | bytes 4194320 | tf_op jit(solution)/shard_map/all_gather | solution.py:87
  75.3 6.2 copy.73
  81.5 7.0 %fusion.48 = (f32[4,8,128]{2,1,0:T(8,128)S(1)}, f32[4,8,128,1024]{3,2,1,0:T(8,128)S(1)}) fusion(f32[8,128,1024]{2,1,0:T(8,128)} %broadcast_multiply_fusion, bf16[4,128,8,64]{1,3,2,0:T(8,128)(2,1)S(1)} %copy.74, bf16[4,1024,8,64]{1,3,2,0:T(8,128)(2,1)} %bitcast.89, pred[4,128,1024]{2,1,0:T(8,128)(4,1)} %compare_and_fusion), kind=kOutput, calls=%fused_computation.107 | convolution fusion | flops 553644032 | bytes 26230784 | tf_op jit(solution)/shard_map/rqhd,rkhd->rhqk/dot_general | solution.py:30
  94.3 29.1 %all-gather.3.cloned.1.call-done = bf16[4,1024,512]{2,1,0:T(8,128)(2,1)} async-done(((bf16[4,128,512]{2,1,0:T(8,128)(2,1)}), bf16[4,1024,512]{2,1,0:T(8,128)(2,1)}) %all-gather.3.cloned.1.call-update) | async-done | bytes 4194320 | tf_op jit(solution)/shard_map/all_gather | solution.py:88
  123.4 6.2 copy.71
  129.6 9.1 %fusion.21 = bf16[4,128,8,64]{1,3,2,0:T(8,128)(2,1)S(1)} fusion(bf16[4,1024,8,64]{1,3,2,0:T(8,128)(2,1)} %bitcast.93, f32[4,8,128,1024]{3,2,1,0:T(8,128)} %copy-done.2, f32[4,8,128]{2,1,0:T(8,128)S(1)} %fusion, f32[4,8,128]{2,1,0:T(8,128)S(1)} %get-tuple-element.52), kind=kOutput, calls=%fused_computation.56 | convolution fusion | flops 549715968 | bytes 21528576 | tf_op jit(solution)/shard_map/rhqk,rkhd->rqhd/dot_general | solution.py:99
  140.7 11.5 %multiply_convert_fusion.2 = (bf16[512,2048]{1,0:T(8,128)(2,1)}, f32[512,2048]{1,0:T(8,128)S(1)}, f32[512,2048]{1,0:T(8,128)S(1)}) fusion(f32[2048]{0:T(1024)S(1)} %copy-done.62, bf16[512,2048]{1,0:T(8,128)(2,1)S(1)} %copy-done, f32[512,512]{0,1:T(8,128)S(1)} %get-tuple-element.55, f32[512]{0:T(512)S(1)} %copy-done.53, f32[512]{0:T(512)S(1)} %copy-done.49, ...), kind=kOutput, calls=%fused_computation.17 | convolution fusion | flops 1144258560 | bytes 13647872 | tf_op jit(solution)/shard_map/dot_general | solution.py:16
  169.3 12.3 %multiply_reduce_fusion.1 = (f32[4,8,128]{2,1,0:T(8,128)S(1)}, f32[4,8,128,1024]{3,2,1,0:T(8,128)}) fusion(f32[4,8,128,1024]{3,2,1,0:T(8,128)} %copy-done.2, f32[4,8,128]{2,1,0:T(8,128)S(1)} %log_add_fusion, bf16[4,128,8,64]{1,3,2,0:T(8,128)(2,1)S(1)} %copy.80, bf16[4,1024,8,64]{1,3,2,0:T(8,128)(2,1)} %bitcast.94), kind=kOutput, calls=%fused_computation.2 | convolution fusion | flops 549449728 | bytes 38305792 | tf_op jit(solution)/shard_map/rqhd,rkhd->rhqk/dot_general | solution.py:138
  181.7 12.7 %multiply_reduce_fusion = (f32[8]{0:T(128)S(1)}, bf16[4,8,128,1024]{3,2,1,0:T(8,128)(2,1)S(1)}) fusion(f32[128,1024]{1,0:T(8,128)S(1)} %copy-done.23, f32[4,8,128,1024]{3,2,1,0:T(8,128)} %get-tuple-element.58, f32[4,8,128]{2,1,0:T(8,128)S(1)} %get-tuple-element.57, f32[4,8,128,1024]{3,2,1,0:T(8,128)} %copy-done.2, f32[4,8,128]{2,1,0:T(8,128)S(1)} %log_add_fusion), kind=kLoop, calls=%fused_computation | loop fusion | flops 29360120 | bytes 42500128 | tf_op jit(solution)/shard_map/reduce_sum | solution.py:143
  194.3 3.7 multiply_convert_fusion.1
  198.9 6.3 copy.83
  205.3 9.4 %fusion.12 = bf16[4,8,64,1024]{3,2,1,0:T(8,128)(2,1)} fusion(bf16[4,128,8,64]{1,3,2,0:T(8,128)(2,1)S(1)} %copy.80, f32[4,8,128,1024]{3,2,1,0:T(8,128)} %copy-done.2, f32[4,8,128]{2,1,0:T(8,128)S(1)} %log_add_fusion), kind=kOutput, calls=%fused_computation.35 | convolution fusion | flops 547356672 | bytes 21512192 | tf_op jit(solution)/shard_map/rhqk,rqhd->rkhd/dot_general | solution.py:148
  214.7 6.3 copy.87
  221.5 7.8 %fusion.20 = bf16[4,128,8,64]{1,3,2,0:T(8,128)(2,1)S(1)} fusion(bf16[4,1024,8,64]{1,3,2,0:T(8,128)(2,1)} %bitcast.90, bf16[4,8,128,1024]{3,2,1,0:T(8,128)(2,1)} %copy-done.3), kind=kOutput, calls=%fused_computation.55 | convolution fusion | flops 537395200 | bytes 13107200 | tf_op jit(solution)/shard_map/rhqk,rkhd->rqhd/dot_general | solution.py:144
  244.2 9.9 %reduce-scatter.3.cloned.1.call-done = bf16[4,128,512]{2,1,0:T(8,128)(2,1)} async-done(((bf16[4,1024,512]{2,1,0:T(8,128)(2,1)}), bf16[4,128,512]{2,1,0:T(8,128)(2,1)}) %reduce-scatter.3.cloned.1.call-update) | async-done | bytes 524304 | tf_op jit(solution)/shard_map/reduce_scatter | solution.py:159
  258.2 46.2 %reduce-scatter.5.cloned.1.call-done = bf16[4,128,512]{2,1,0:T(8,128)(2,1)} async-done(((bf16[4,1024,512]{2,1,0:T(8,128)(2,1)}), bf16[4,128,512]{2,1,0:T(8,128)(2,1)}) %reduce-scatter.5.cloned.1.call-update) | async-done | bytes 524304 | tf_op jit(solution)/shard_map/reduce_scatter | solution.py:162
  315.3 4.1 convolution_add_fusion
  319.4 4.9 reshape.222
  326.9 4.8 reshape.225
  339.8 41.8 %all-reduce = (f32[512]{0:T(512)}, f32[512]{0:T(512)}, f32[512]{0:T(512)}, f32[8]{0:T(128)}, f32[512]{0:T(512)}, /*index=5*/f32[512]{0:T(512)}, f32[2048]{0:T(1024)}, f32[512]{0:T(512)}, f32[1536]{0:T(1024)}) all-reduce(f32[512]{0:T(512)S(1)} %get-tuple-element.44, ...), channel_id=1, replica_groups=mesh['batch'=4,'seq'=8] {'batch','seq'}, use_global_device_ids=true, to_apply=%region_17.18 | all-reduce | flops 6664 | bytes 53312 | tf_op jit(solution)/shard_map/psum | solution.py:202
  381.6 4.2 maximum_add_fusion
  385.8 236.1 %all-reduce.4.cloned.1.call-done = (f32[1536,512]{1,0:T(8,128)}, f32[512,512]{1,0:T(8,128)}, f32[512,512]{1,0:T(8,128)}, f32[512,512]{1,0:T(8,128)}, f32[512,512...) async-done(((f32[1536,512]{1,0:T(8,128)}, f32[512,512]{1,0:T(8,128)}, f32[512,512]{1,0:T(8,128)}, f32[512,512]{1,0:T(8,128)}, ...) | async-done | bytes 18874384 | tf_op jit(solution)/shard_map/psum | solution.py:202
  621.9 4.0 copy.128
  (218 shorter events, 113.5 us)
Async XLA Ops:
  7.2 133.5 %copy-start = (bf16[512,2048]{1,0:T(8,128)(2,1)S(1)}, bf16[512,2048]{1,0:T(8,128)(2,1)}, u32[]{:S(2)}) copy-start(bf16[512,2048]{1,0:T(8,128)(2,1)} %param.34) | copy-start | bytes 6291460
  7.2 10.8 %copy-start.64 = (f32[512]{0:T(512)S(1)}, f32[512]{0:T(512)}, u32[]{:S(2)}) copy-start(f32[512]{0:T(512)} %param.24) | copy-start | bytes 6148
  7.2 68.1 %all-gather.5.cloned.1.call-start = ((), (), s32[]{:S(2)}) async-start(), calls=%async_computation.3 | async-start | bytes 4718592 | tf_op jit(solution)/shard_map/all_gather | solution.py:87
  8.2 3.2 collective-permute-start
  21.2 8.1 %copy-start.54 = (f32[512]{0:T(512)}, f32[512]{0:T(512)S(1)}, u32[]{:S(2)}) copy-start(f32[512]{0:T(512)S(1)} %multiply_reduce_fusion.7) | copy-start | bytes 6148
  22.2 18.5 %copy-start.16 = (bf16[512,512]{0,1:T(8,128)(2,1)}, bf16[512,512]{0,1:T(8,128)(2,1)S(1)}, u32[]{:S(2)}) copy-start(bf16[512,512]{0,1:T(8,128)(2,1)S(1)} %add_convert_fusion.4) | copy-start | bytes 1572868
  23.5 99.9 %all-gather.3.cloned.1.call-start = ((), (), s32[]{:S(2)}) async-start(), calls=%async_computation.2 | async-start | bytes 4718592 | tf_op jit(solution)/shard_map/all_gather | solution.py:88
  24.9 229.2 %reduce-scatter.3.cloned.1.call-start = ((), (), s32[]{:S(2)}) async-start(), calls=%async_computation.4 | async-start | bytes 4718592 | tf_op jit(solution)/shard_map/reduce_scatter | solution.py:159
  29.3 8.8 %copy-start.59 = (f32[8]{0:T(128)S(1)}, f32[8]{0:T(128)}, u32[]{:S(2)}) copy-start(f32[8]{0:T(128)} %param.31) | copy-start | bytes 100
  46.1 35.4 %copy-start.20 = (bf16[4,128,8,64]{1,3,2,0:T(8,128)(2,1)}, bf16[4,128,8,64]{1,3,2,0:T(8,128)(2,1)S(1)}, u32[]{:S(2)}) copy-start(bf16[4,128,8,64]{1,3,2,0:T(8,128)(2,1)S(1)} %copy.74) | copy-start | bytes 1572868
  129.6 10.4 %copy-start.5 = (f32[512,512]{0,1:T(8,128)S(1)}, f32[512,512]{0,1:T(8,128)}, u32[]{:S(2)}) copy-start(f32[512,512]{0,1:T(8,128)} %copy-done.4) | copy-start | bytes 3145732
  129.6 10.4 %copy-start.34 = (bf16[512,512]{1,0:T(8,128)(2,1)S(1)}, bf16[512,512]{1,0:T(8,128)(2,1)}, u32[]{:S(2)}) copy-start(bf16[512,512]{1,0:T(8,128)(2,1)} %param.30) | copy-start | bytes 1572868
  140.5 11.8 %copy-start.6 = (f32[512,512]{0,1:T(8,128)}, f32[512,512]{0,1:T(8,128)S(1)}, u32[]{:S(2)}) copy-start(f32[512,512]{0,1:T(8,128)S(1)} %get-tuple-element.55) | copy-start | bytes 3145732
  140.7 11.5 %copy-start.28 = (f32[512,512]{1,0:T(8,128)S(1)}, f32[512,512]{1,0:T(8,128)}, u32[]{:S(2)}) copy-start(f32[512,512]{1,0:T(8,128)} %get-tuple-element.65) | copy-start | bytes 3145732
  140.7 11.5 %copy-start.60 = (bf16[2048,512]{1,0:T(8,128)(2,1)S(1)}, bf16[2048,512]{1,0:T(8,128)(2,1)}, u32[]{:S(2)}) copy-start(bf16[2048,512]{1,0:T(8,128)(2,1)} %param.36) | copy-start | bytes 6291460
  169.3 12.3 %copy-start.23 = (f32[128,1024]{1,0:T(8,128)S(1)}, f32[128,1024]{1,0:T(8,128)}, u32[]{:S(2)}) copy-start(f32[128,1024]{1,0:T(8,128)} %copy-done.22) | copy-start | bytes 1572868
  181.7 12.7 %copy-start.21 = (bf16[4,128,8,64]{1,3,2,0:T(8,128)(2,1)S(1)}, bf16[4,128,8,64]{1,3,2,0:T(8,128)(2,1)}, u32[]{:S(2)}) copy-start(bf16[4,128,8,64]{1,3,2,0:T(8,128)(2,1)} %copy-done.20) | copy-start | bytes 1572868
  205.2 99.2 %reduce-scatter.5.cloned.1.call-start = ((), (), s32[]{:S(2)}) async-start(), calls=%async_computation.5 | async-start | bytes 4718592 | tf_op jit(solution)/shard_map/reduce_scatter | solution.py:162
  221.0 10.3 %copy-start.17 = (bf16[512,512]{0,1:T(8,128)(2,1)S(1)}, bf16[512,512]{0,1:T(8,128)(2,1)}, u32[]{:S(2)}) copy-start(bf16[512,512]{0,1:T(8,128)(2,1)} %copy-done.16) | copy-start | bytes 1572868
  221.0 400.9 %all-reduce.4.cloned.1.call-start = ((), (), s32[]{:S(2)}) async-start(), calls=%async_computation.6 | async-start | bytes 37748736 | tf_op jit(solution)/shard_map/psum | solution.py:202
  221.5 8.3 %copy-start.25 = (bf16[512,512]{0,1:T(8,128)(2,1)S(1)}, bf16[512,512]{0,1:T(8,128)(2,1)}, u32[]{:S(2)}) copy-start(bf16[512,512]{0,1:T(8,128)(2,1)} %copy-done.24) | copy-start | bytes 1572868
  221.5 8.3 %copy-start.27 = (bf16[4,128,8,64]{1,0,3,2:T(4,128)(2,1)S(1)}, bf16[4,128,8,64]{1,0,3,2:T(4,128)(2,1)}, u32[]{:S(2)}) copy-start(bf16[4,128,8,64]{1,0,3,2:T(4,128)(2,1)} %copy-done.26) | copy-start | bytes 1572868
  332.7 49.0 %collective-permute-start.1 = (f32[4,2,512]{2,1,0:T(2,128)S(1)}, f32[4,2,512]{2,1,0:T(2,128)S(1)}, u32[]{:S(2)}, u32[]{:S(2)}) collective-permute-start(f32[4,2,512]{2,1,0:T(2,128)S(1)} %slice.17), channel_id=1, source_target_pairs={{1,0},{2,1},{3,2},{4,3},{5,4},{6,5},{7,6},{9,8},{10,9},{11,10},{12... | collective-permute-start | bytes 49160 | tf_op jit(solution)/shard_map/ppermute | solution.py:12
  337.7 43.9 %copy-start.19 = (bf16[4,384,512]{2,1,0:T(8,128)(2,1)S(1)}, bf16[4,384,512]{2,1,0:T(8,128)(2,1)}, u32[]{:S(2)}) copy-start(bf16[4,384,512]{2,1,0:T(8,128)(2,1)} %param.21) | copy-start | bytes 4718596
  (49 other events, 169.2 us)
Sparse Core Ops, SparseCore 0:
  23.6 51.6 all-gather.4
  77.5 45.8 all-gather.2
  205.3 48.7 reduce-scatter.2
  256.3 48.1 reduce-scatter.4
  313.7 308.0 all-reduce.3
where the time goes:
time: 650 us; the launch traced here: 645 us
  waiting for transfers between devices  351 us (54%)
  matrix products  110 us (17%)
  local copies, waits for them, and re-layouts  84.8 us (13%)
  blocking collectives  41.8 us (6%)
  other arithmetic  37.2 us (6%)
  between operations  14.6 us (2%)
    psum x1, waiting for transfers between devices, local(): lax.psum((local_grads[0], local_grads[1], local_grads[2], local_grads[3],...  236 us
    dot_general x24, matrix products, matmul(): return jnp.dot(left, right, preferred_element_type=jnp.float32)  61 us
    reduce_scatter x1, waiting for transfers between devices, local(): lax.psum_scatter(grad_value_term.astype(jnp.bfloat16), 'seq', scatter_dim...  46.2 us
    psum x1, blocking collectives, local(): lax.psum((local_grads[0], local_grads[1], local_grads[2], local_grads[3],...  41.8 us
    all_gather x1, waiting for transfers between devices, local(): lax.all_gather(key_block, 'seq', axis=1, tiled=True)  29.2 us
    all_gather x1, waiting for transfers between devices, local(): lax.all_gather(value_block, 'seq', axis=1, tiled=True)  29.1 us
    unnamed x140, local copies, waits for them, and re-layouts  25.4 us
  transfers between devices with their start and end apart: 7, of which 6 were waited for; matrix products, arithmetic and copies ran while one was open for 17% of the time, Pallas kernels for 0%

commit v1 on v0

--- a/solution.py
+++ b/solution.py
@@ -1,9 +1,301 @@
+import functools
+import math
+
 import jax
 import jax.numpy as jnp
 from jax import lax
+from jax.experimental import pallas as pl
+from jax.experimental.pallas import tpu as pltpu
 from jax.sharding import PartitionSpec as P
 
 norm_eps = 1e-05
+
+MESH = pl.DeviceIdType.MESH
+half = jnp.bfloat16
+full = jnp.float32
+
+
+class Place:
+    def __init__(self, batch_size, seq_size):
+        side = math.isqrt(batch_size)
+        self.depth = seq_size // 2
+        self.batch = lax.axis_index("batch")
+        self.seq = lax.axis_index("seq")
+        self.core = self.seq % 2
+        self.level = self.seq // 2
+        high, low = self.batch // side, self.batch % side
+        self.first = jnp.where(self.core == 0, low, high)
+        self.second = jnp.where(self.core == 0, high, low)
+        self.side = side
+        self.sizes = (2, side, side, self.depth)
+        self.where = (self.core, self.first, self.second, self.level)
+
+    def batch_at(self, first, second):
+        return jnp.where(
+            self.core == 0, second * self.side + first, first * self.side + second
+        )
+
+    def partner(self, stage, step):
+        member = (self.where[stage] + step) % self.sizes[stage]
+        if stage == 0:
+            return (self.batch, self.level * 2 + member)
+        if stage == 1:
+            return (self.batch_at(member, self.second), self.seq)
+        if stage == 2:
+            return (self.batch_at(self.first, member), self.seq)
+        return (self.batch, member * 2 + self.core)
+
+    def partners(self):
+        return [
+            self.partner(stage, step)
+            for stage in range(4)
+            for step in range(1, self.sizes[stage])
+        ]
+
+
+def sum_slots(batch_size, seq_size):
+    return 1 + 2 * (math.isqrt(batch_size) - 1) + seq_size // 2 - 1
+
+
+class SumPieces:
+    def __init__(self, place, chunks, mine, landing, out, sems):
+        self.place, self.chunks = place, chunks
+        self.mine, self.landing, self.out = mine, landing, out
+        self.sent, self.got, self.back_sent, self.back_got = sems
+        self.starts = [sum(chunks[:c]) for c in range(len(chunks))]
+        sizes = place.sizes
+        self.slot = [sum(s - 1 for s in sizes[:stage]) for stage in range(4)]
+        self.land = {}
+        at = 0
+        for c in range(len(chunks)):
+            for stage in range(4):
+                for step in range(1, sizes[stage]):
+                    self.land[c, stage, step] = at
+                    at += self.rows(c, stage)
+
+    @staticmethod
+    def landing_rows(batch_size, seq_size, chunks):
+        side = math.isqrt(batch_size)
+        rows, left = 0, sum(chunks)
+        for size in (2, side, side, seq_size // 2):
+            left //= size
+            rows += left * (size - 1)
+        return rows
+
+    def rows(self, c, stage):
+        count = self.chunks[c]
+        for size in self.place.sizes[: stage + 1]:
+            count //= size
+        return count
+
+    def begin(self, c, stage):
+        at = self.starts[c]
+        for t in range(stage):
+            at = at + self.place.where[t] * self.rows(c, t)
+        return at
+
+    def scatter(self, c, stage, step):
+        count = self.rows(c, stage)
+        member = (self.place.where[stage] + step) % self.place.sizes[stage]
+        at = pl.multiple_of(self.begin(c, stage) + member * count, 16)
+        slot = self.slot[stage] + step - 1
+        return pltpu.make_async_remote_copy(
+            src_ref=self.mine.at[pl.ds(at, count), :],
+            dst_ref=self.landing.at[pl.ds(self.land[c, stage, step], count), :],
+            send_sem=self.sent.at[c, slot],
+            recv_sem=self.got.at[c, slot],
+            device_id=self.place.partner(stage, step),
+            device_id_type=MESH,
+        )
+
+    def gather(self, c, stage, step):
+        count = self.rows(c, stage)
+        at = pl.multiple_of(self.begin(c, stage + 1), 16)
+        slot = self.slot[stage] + step - 1
+        return pltpu.make_async_remote_copy(
+            src_ref=self.out.at[pl.ds(at, count), :],
+            dst_ref=self.out.at[pl.ds(at, count), :],
+            send_sem=self.back_sent.at[c, slot],
+            recv_sem=self.back_got.at[c, slot],
+            device_id=self.place.partner(stage, step),
+            device_id_type=MESH,
+        )
+
+    def add(self, c, stage):
+        count = self.rows(c, stage)
+        at = self.begin(c, stage + 1)
+        target = self.out if stage == 3 else self.mine
+        part = min(count, 128)
+
+        def body(i, carry):
+            here = pl.multiple_of(at + i * part, 16)
+            total = self.mine[pl.ds(here, part), :].astype(full)
+            for step in range(1, self.place.sizes[stage]):
+                there = pl.multiple_of(self.land[c, stage, step] + i * part, 16)
+                total = total + self.landing[pl.ds(there, part), :].astype(full)
+            target[pl.ds(here, part), :] = total.astype(half)
+            return carry
+
+        lax.fori_loop(0, count // part, body, 0)
+
+    def steps(self, stage):
+        return range(1, self.place.sizes[stage])
+
+    def advance(self, c, event):
+        if 1 <= event <= 4:
+            for step in self.steps(event - 1):
+                self.scatter(c, event - 1, step).wait_recv()
+            self.add(c, event - 1)
+        if event <= 3:
+            for step in self.steps(event):
+                self.scatter(c, event, step).start()
+        else:
+            stage = 7 - event
+            if event >= 5:
+                for step in self.steps(stage + 1):
+                    self.gather(c, stage + 1, step).wait_recv()
+            if event <= 7:
+                for step in self.steps(stage):
+                    self.gather(c, stage, step).start()
+
+    def finish(self):
+        for c in range(len(self.chunks)):
+            for stage in range(4):
+                for step in self.steps(stage):
+                    self.scatter(c, stage, step).wait_send()
+                    self.gather(c, stage, step).wait_send()
+
+
+class SumSmall:
+    def __init__(self, place, block, landing, sems):
+        self.place, self.block, self.landing = place, block, landing
+        self.sent, self.got = sems
+        sizes = place.sizes
+        self.slot = [sum(s - 1 for s in sizes[:stage]) for stage in range(4)]
+        self.base = [sum(sizes[:stage]) for stage in range(4)]
+
+    def copy(self, stage, step):
+        slot = self.slot[stage] + step - 1
+        return pltpu.make_async_remote_copy(
+            src_ref=self.block.at[stage],
+            dst_ref=self.landing.at[self.base[stage] + self.place.where[stage]],
+            send_sem=self.sent.at[slot],
+            recv_sem=self.got.at[slot],
+            device_id=self.place.partner(stage, step),
+            device_id_type=MESH,
+        )
+
+    def send(self, stage):
+        self.landing[self.base[stage] + self.place.where[stage]] = self.block[stage]
+        for step in range(1, self.place.sizes[stage]):
+            self.copy(stage, step).start()
+
+    def receive(self, stage):
+        for step in range(1, self.place.sizes[stage]):
+            self.copy(stage, step).wait_recv()
+        total = self.landing[self.base[stage]]
+        for member in range(1, self.place.sizes[stage]):
+            total = total + self.landing[self.base[stage] + member]
+        self.block[stage + 1] = total
+
+    def finish(self):
+        for stage in range(4):
+            for step in range(1, self.place.sizes[stage]):
+                self.copy(stage, step).wait_send()
+
+
+def sum_kernel(batch_size, seq_size, chunks, lag, big_ref, small_ref, big_out, small_out,
+               mine, landing, small_block, small_landing, *sems):
+    place = Place(batch_size, seq_size)
+    barrier = pltpu.get_barrier_semaphore()
+    partners = place.partners()
+    for device in partners:
+        pl.semaphore_signal(barrier, inc=1, device_id=device, device_id_type=MESH)
+    pl.semaphore_wait(barrier, len(partners))
+    load = pltpu.make_async_copy(big_ref, mine, sems[6])
+    load.start()
+    small_block[0] = small_ref[...]
+    small = SumSmall(place, small_block, small_landing, sems[4:6])
+    big = SumPieces(place, chunks, mine, landing, big_out, sems[:4])
+    load.wait()
+    for t in range(len(chunks) + 8 * lag):
+        for event in reversed(range(9)):
+            c = t - event * lag
+            if 0 <= c < len(chunks):
+                big.advance(c, event)
+        if t % 2 == 0 and t // 2 <= 4:
+            if t >= 2:
+                small.receive(t // 2 - 1)
+            if t // 2 < 4:
+                small.send(t // 2)
+    small_out[...] = small_block[4]
+    big.finish()
+    small.finish()
+
+
+def sum_over_devices(big, small):
+    batch_size, seq_size = lax.axis_size("batch"), lax.axis_size("seq")
+    rows = big.shape[0]
+    chunks = [4096] * (rows // 4096)
+    slots = sum_slots(batch_size, seq_size)
+    small_rows = small.shape[0]
+    members = 2 + 2 * math.isqrt(batch_size) + seq_size // 2
+    vmem = pl.BlockSpec(memory_space=pltpu.VMEM)
+    return pl.pallas_call(
+        functools.partial(sum_kernel, batch_size, seq_size, chunks, 2),
+        out_shape=(
+            jax.ShapeDtypeStruct(big.shape, half),
+            jax.ShapeDtypeStruct(small.shape, full),
+        ),
+        in_specs=[pl.BlockSpec(memory_space=pl.ANY), vmem],
+        out_specs=(vmem, vmem),
+        scratch_shapes=[
+            pltpu.VMEM(big.shape, half),
+            pltpu.VMEM((SumPieces.landing_rows(batch_size, seq_size, chunks), 128), half),
+            pltpu.VMEM((5, small_rows, 128), full),
+            pltpu.VMEM((members, small_rows, 128), full),
+        ]
+        + [pltpu.SemaphoreType.DMA((len(chunks), slots))] * 4
+        + [pltpu.SemaphoreType.DMA((slots,))] * 2
+        + [pltpu.SemaphoreType.DMA],
+        compiler_params=pltpu.CompilerParams(
+            collective_id=0, has_side_effects=True, vmem_limit_bytes=60 * 1024 * 1024
+        ),
+        name="sum_over_devices",
+    )(big, small)
+
+
+def sum_grads(grads):
+    big_names = [i for i, g in enumerate(grads) if g.ndim == 2]
+    small_names = [i for i, g in enumerate(grads) if g.ndim == 1]
+    big = jnp.concatenate(
+        [
+            grads[i][:, j : j + 128].astype(half)
+            for i in big_names
+            for j in range(0, grads[i].shape[1], 128)
+        ],
+        axis=0,
+    )
+    flat = jnp.concatenate([grads[i] for i in small_names])
+    small_rows = -(-flat.shape[0] // 1024) * 8
+    flat = jnp.pad(flat, (0, small_rows * 128 - flat.shape[0])).reshape(small_rows, 128)
+    big, flat = sum_over_devices(big, flat)
+    flat = flat.reshape(-1)
+    out = list(grads)
+    at = 0
+    for i in big_names:
+        rows, columns = grads[i].shape
+        parts = []
+        for j in range(columns // 128):
+            parts.append(big[at : at + rows].astype(full))
+            at += rows
+        out[i] = jnp.concatenate(parts, axis=1)
+    at = 0
+    for i in small_names:
+        count = grads[i].shape[0]
+        out[i] = flat[at : at + count]
+        at += count
+    return tuple(out)
 
 
 def shifted_2(block, axis, distance):
@@ -199,28 +491,7 @@
         grad_up_weight,
         grad_up_bias,
     )
-    summed = lax.psum(
-        (
-            local_grads[0],
-            local_grads[1],
-            local_grads[2],
-            local_grads[3],
-            local_grads[4],
-            local_grads[5],
-            local_grads[6],
-            local_grads[7],
-            local_grads[8],
-            local_grads[9],
-            local_grads[10],
-            local_grads[11],
-            local_grads[12],
-            local_grads[13],
-            local_grads[14],
-            local_grads[15],
-            local_grads[16],
-        ),
-        ("batch", "seq"),
-    )
+    summed = sum_grads(local_grads)
     return (output, input_grad) + tuple(summed)
 
 

time: 650 us -> 526 us (0.81)
  waiting for transfers between devices: 351 us -> 99.3 us
  Pallas kernels: 0 us -> 93.9 us
  local copies, waits for them, and re-layouts: 84.8 us -> 139 us
  blocking collectives: 41.8 us -> 0 us
  other arithmetic: 37.2 us -> 48.9 us
  matrix products: 110 us -> 121 us
    psum x1 -> x0, waiting for transfers between devices: 236 us -> none  [local(): lax.psum((local_grads[0], local_grads[1], local_grads[2], local_grads[3],...]
    pallas_call x0 -> x1, Pallas kernels: none -> 93.9 us  [sum_over_devices(): pl.pallas_call(functools.partial(sum_kernel, batch_size, seq_size, chunks...]
    unnamed x140 -> x208, local copies, waits for them, and re-layouts: 25.4 us -> 68.1 us
    psum x1 -> x0, blocking collectives: 41.8 us -> none  [local(): lax.psum((local_grads[0], local_grads[1], local_grads[2], local_grads[3],...]
    concatenate x0 -> x6, other arithmetic: none -> 13.4 us  [sum_grads(): out[i] = jnp.concatenate(parts, axis=1)]
    reduce_scatter x1, waiting for transfers between devices: 9.88 us -> 0.01 us  [local(): lax.psum_scatter(grad_key_term.astype(jnp.bfloat16), 'seq', scatter_dimen...]
    slice x0 -> x7, local copies, waits for them, and re-layouts: none -> 7.24 us  [the longest x2 4.14 us: sum_grads(): parts.append(big[at:at + rows].astype(full))]
  transfers between devices with their start and end apart: 7 -> 6, of which waited for: 6 -> 4; matrix products, arithmetic and copies ran while one was open for 17% -> 25% of each run, Pallas kernels for 0% -> 0%
where the time goes in v1:
time: 526 us; the launch traced here: 521 us
  local copies, waits for them, and re-layouts  139 us (26%)
  matrix products  121 us (23%)
  waiting for transfers between devices  99.3 us (19%)
  Pallas kernels  93.9 us (18%)
  other arithmetic  48.9 us (9%)
  between operations  14.7 us (3%)
    pallas_call x1, Pallas kernels, sum_over_devices(): pl.pallas_call(functools.partial(sum_kernel, batch_size, seq_size, chunks...  93.9 us
    unnamed x208, local copies, waits for them, and re-layouts  68.1 us
    dot_general x24, matrix products, matmul(): return jnp.dot(left, right, preferred_element_type=jnp.float32)  64.1 us
    reduce_scatter x1, waiting for transfers between devices, local(): lax.psum_scatter(grad_value_term.astype(jnp.bfloat16), 'seq', scatter_dim...  39.9 us
    all_gather x1, waiting for transfers between devices, local(): lax.all_gather(key_block, 'seq', axis=1, tiled=True)  29.4 us
    all_gather x1, waiting for transfers between devices, local(): lax.all_gather(value_block, 'seq', axis=1, tiled=True)  29.1 us
    dot_general x1, matrix products, local(): jnp.einsum('rqhd,rkhd->rhqk', grad_heads, value_heads, preferred_element_...  16.8 us
    concatenate x6, other arithmetic, sum_grads(): out[i] = jnp.concatenate(parts, axis=1)  13.4 us
  transfers between devices with their start and end apart: 6, of which 4 were waited for; matrix products, arithmetic and copies ran while one was open for 25% of the time, Pallas kernels for 0%

profile of v1, /device:TPU:0, one launch (start us, length us, event | category | flops | bytes accessed | tf_op | source)
XLA Modules:
  0.0 520.7 jit_solution(9027081857011740617)
XLA Ops:
  14.3 3.7 reshape.225
  25.4 3.7 reshape.232
  29.1 4.4 convert_reduce_fusion.2
  45.9 29.4 %all-gather.5.cloned.1.call-done = bf16[4,1024,512]{2,1,0:T(8,128)(2,1)} async-done(((bf16[4,128,512]{2,1,0:T(8,128)(2,1)}), bf16[4,1024,512]{2,1,0:T(8,128)(2,1)}) %all-gather.5.cloned.1.call-update) | async-done | bytes 4194320 | tf_op jit(solution)/shard_map/all_gather | solution.py:379
  75.3 6.2 %copy.73 = bf16[4,1024,512]{1,2,0:T(8,128)(2,1)} copy(bf16[4,1024,512]{2,1,0:T(8,128)(2,1)} %all-gather.5.cloned.1.call-done) | data formatting | bytes 8388608 | tf_op jit(solution)/shard_map/all_gather | solution.py:379
  81.5 7.0 %fusion.47 = (f32[4,8,128]{2,1,0:T(8,128)S(1)}, f32[4,8,128,1024]{3,2,1,0:T(8,128)S(1)}) fusion(f32[8,128,1024]{2,1,0:T(8,128)} %broadcast_multiply_fusion, bf16[4,128,8,64]{1,3,2,0:T(8,128)(2,1)S(1)} %copy.74, bf16[4,1024,8,64]{1,3,2,0:T(8,128)(2,1)} %bitcast.98, pred[4,128,1024]{2,1,0:T(8,128)(4,1)} %compare_and_fusion), kind=kOutput, calls=%fused_computation.204 | convolution fusion | flops 553644032 | bytes 26230784 | tf_op jit(solution)/shard_map/rqhd,rkhd->rhqk/dot_general | solution.py:322
  88.6 3.7 fusion
  94.3 29.1 %all-gather.3.cloned.1.call-done = bf16[4,1024,512]{2,1,0:T(8,128)(2,1)} async-done(((bf16[4,128,512]{2,1,0:T(8,128)(2,1)}), bf16[4,1024,512]{2,1,0:T(8,128)(2,1)}) %all-gather.3.cloned.1.call-update) | async-done | bytes 4194320 | tf_op jit(solution)/shard_map/all_gather | solution.py:380
  123.4 6.2 %copy.71 = bf16[4,1024,512]{1,2,0:T(8,128)(2,1)} copy(bf16[4,1024,512]{2,1,0:T(8,128)(2,1)} %all-gather.3.cloned.1.call-done) | data formatting | bytes 8388608 | tf_op jit(solution)/shard_map/all_gather | solution.py:380
  129.6 9.4 %fusion.21 = bf16[4,128,8,64]{1,3,2,0:T(8,128)(2,1)S(1)} fusion(bf16[4,1024,8,64]{1,3,2,0:T(8,128)(2,1)} %bitcast.102, f32[4,8,128,1024]{3,2,1,0:T(8,128)} %copy-done.2, f32[4,8,128]{2,1,0:T(8,128)S(1)} %fusion, f32[4,8,128]{2,1,0:T(8,128)S(1)} %get-tuple-element.93), kind=kOutput, calls=%fused_computation.66 | convolution fusion | flops 549715968 | bytes 21528576 | tf_op jit(solution)/shard_map/rhqk,rkhd->rqhd/dot_general | solution.py:391
  140.6 11.5 %multiply_convert_fusion.2 = (bf16[512,2048]{1,0:T(8,128)(2,1)}, f32[512,2048]{1,0:T(8,128)S(1)}, f32[512,2048]{1,0:T(8,128)S(1)}) fusion(f32[2048]{0:T(1024)S(1)} %copy-done.61, bf16[512,2048]{1,0:T(8,128)(2,1)S(1)} %copy-done, f32[512,512]{0,1:T(8,128)S(1)} %get-tuple-element.96, f32[512]{0:T(512)S(1)} %copy-done.65, f32[512]{0:T(512)S(1)} %copy-done.53, ...), kind=kOutput, calls=%fused_computation.17 | convolution fusion | flops 1144258560 | bytes 13647872 | tf_op jit(solution)/shard_map/dot_general | solution.py:308
  171.7 16.8 %multiply_reduce_fusion.1 = (f32[4,8,128]{2,1,0:T(8,128)S(1)}, f32[4,8,128,1024]{3,2,1,0:T(8,128)}) fusion(f32[4,8,128,1024]{3,2,1,0:T(8,128)} %copy-done.2, f32[4,8,128]{2,1,0:T(8,128)S(1)} %log_add_fusion, bf16[4,128,8,64]{1,3,2,0:T(8,128)(2,1)} %copy.80, bf16[4,1024,8,64]{1,3,2,0:T(8,128)(2,1)} %bitcast.103), kind=kOutput, calls=%fused_computation.2 | convolution fusion | flops 549449728 | bytes 38305792 | tf_op jit(solution)/shard_map/rqhd,rkhd->rhqk/dot_general | solution.py:430
  188.5 12.7 %multiply_reduce_fusion = (f32[8]{0:T(128)S(1)}, bf16[4,8,128,1024]{3,2,1,0:T(8,128)(2,1)S(1)}) fusion(f32[128,1024]{1,0:T(8,128)S(1)} %copy-done.18, f32[4,8,128,1024]{3,2,1,0:T(8,128)} %get-tuple-element.99, f32[4,8,128]{2,1,0:T(8,128)S(1)} %get-tuple-element.98, f32[4,8,128,1024]{3,2,1,0:T(8,128)} %copy-done.2, f32[4,8,128]{2,1,0:T(8,128)S(1)} %log_add_fusion), kind=kLoop, calls=%fused_computation | loop fusion | flops 29360120 | bytes 42500128 | tf_op jit(solution)/shard_map/reduce_sum | solution.py:435
  201.2 3.7 multiply_convert_fusion.1
  205.7 6.4 %copy.83 = bf16[4,1024,512]{2,1,0:T(8,128)(2,1)} copy(bf16[4,1024,512]{1,2,0:T(8,128)(2,1)} %bitcast.101) | data formatting | bytes 8388608 | tf_op jit(solution)/shard_map/convert_element_type | solution.py:452
  212.2 11.5 %fusion.12 = bf16[4,8,64,1024]{3,2,1,0:T(8,128)(2,1)} fusion(bf16[4,128,8,64]{1,3,2,0:T(8,128)(2,1)} %copy.80, f32[4,8,128,1024]{3,2,1,0:T(8,128)} %copy-done.2, f32[4,8,128]{2,1,0:T(8,128)S(1)} %log_add_fusion), kind=kOutput, calls=%fused_computation.39 | convolution fusion | flops 547356672 | bytes 21512192 | tf_op jit(solution)/shard_map/rhqk,rqhd->rkhd/dot_general | solution.py:440
  223.7 6.2 %copy.87 = bf16[4,1024,512]{2,1,0:T(8,128)(2,1)} copy(bf16[4,1024,512]{1,2,0:T(8,128)(2,1)} %bitcast.100) | data formatting | bytes 8388608 | tf_op jit(solution)/shard_map/convert_element_type | solution.py:455
  231.6 7.9 %fusion.20 = bf16[4,128,8,64]{1,3,2,0:T(8,128)(2,1)S(1)} fusion(bf16[4,1024,8,64]{1,3,2,0:T(8,128)(2,1)} %bitcast.99, bf16[4,8,128,1024]{3,2,1,0:T(8,128)(2,1)} %copy-done.3), kind=kOutput, calls=%fused_computation.65 | convolution fusion | flops 537395200 | bytes 13107200 | tf_op jit(solution)/shard_map/rhqk,rkhd->rqhd/dot_general | solution.py:436
  245.6 5.0 reshape.231
  255.8 3.7 convolution_convert_fusion
  271.5 39.9 %reduce-scatter.5.cloned.1.call-done = bf16[4,128,512]{2,1,0:T(8,128)(2,1)} async-done(((bf16[4,1024,512]{2,1,0:T(8,128)(2,1)}), bf16[4,128,512]{2,1,0:T(8,128)(2,1)}) %reduce-scatter.5.cloned.1.call-update) | async-done | bytes 524304 | tf_op jit(solution)/shard_map/reduce_scatter | solution.py:454
  359.3 93.9 %sum_over_devices.1 = (bf16[36864,128]{1,0:T(8,128)(2,1)}, f32[56,128]{1,0:T(8,128)}) custom-call(bf16[36864,128]{1,0:T(8,128)(2,1)} %constant_dynamic-update-slice_fusion.big_ref, f32[56,128]{1,0:T(8,128)} %pad_bitcast_fusion.small_ref), custom_call_target="tpu_custom_call" | custom-call | tf_op jit(solution)/shard_map/sum_over_devices/pallas_call | solution.py:244
  469.4 4.6 reshape.234
  505.4 4.3 concatenate.75
  (300 shorter events, 175.0 us)
Async XLA Ops:
  7.2 133.4 %copy-start = (bf16[512,2048]{1,0:T(8,128)(2,1)S(1)}, bf16[512,2048]{1,0:T(8,128)(2,1)}, u32[]{:S(2)}) copy-start(bf16[512,2048]{1,0:T(8,128)(2,1)} %param.34) | copy-start | bytes 6291460
  7.2 10.8 %copy-start.63 = (f32[512]{0:T(512)S(1)}, f32[512]{0:T(512)}, u32[]{:S(2)}) copy-start(f32[512]{0:T(512)} %param.24) | copy-start | bytes 6148
  7.2 68.1 %all-gather.5.cloned.1.call-start = ((), (), s32[]{:S(2)}) async-start(), calls=%async_computation.3 | async-start | bytes 4718592 | tf_op jit(solution)/shard_map/all_gather | solution.py:379
  8.2 3.2 collective-permute-start
  22.2 18.3 %copy-start.19 = (bf16[512,512]{0,1:T(8,128)(2,1)}, bf16[512,512]{0,1:T(8,128)(2,1)S(1)}, u32[]{:S(2)}) copy-start(bf16[512,512]{0,1:T(8,128)(2,1)S(1)} %add_convert_fusion.4) | copy-start | bytes 1572868
  23.5 99.9 %all-gather.3.cloned.1.call-start = ((), (), s32[]{:S(2)}) async-start(), calls=%async_computation.2 | async-start | bytes 4718592 | tf_op jit(solution)/shard_map/all_gather | solution.py:380
  24.9 241.7 %reduce-scatter.3.cloned.1.call-start = ((), (), s32[]{:S(2)}) async-start(), calls=%async_computation.4 | async-start | bytes 4718592 | tf_op jit(solution)/shard_map/reduce_scatter | solution.py:451
  45.9 35.6 %copy-start.15 = (bf16[4,128,8,64]{1,3,2,0:T(8,128)(2,1)}, bf16[4,128,8,64]{1,3,2,0:T(8,128)(2,1)S(1)}, u32[]{:S(2)}) copy-start(bf16[4,128,8,64]{1,3,2,0:T(8,128)(2,1)S(1)} %copy.74) | copy-start | bytes 1572868
  129.6 9.9 %copy-start.5 = (f32[512,512]{0,1:T(8,128)S(1)}, f32[512,512]{0,1:T(8,128)}, u32[]{:S(2)}) copy-start(f32[512,512]{0,1:T(8,128)} %copy-done.4) | copy-start | bytes 3145732
  129.6 9.9 %copy-start.27 = (bf16[512,512]{1,0:T(8,128)(2,1)S(1)}, bf16[512,512]{1,0:T(8,128)(2,1)}, u32[]{:S(2)}) copy-start(bf16[512,512]{1,0:T(8,128)(2,1)} %param.30) | copy-start | bytes 1572868
  140.3 11.8 %copy-start.6 = (f32[512,512]{0,1:T(8,128)}, f32[512,512]{0,1:T(8,128)S(1)}, u32[]{:S(2)}) copy-start(f32[512,512]{0,1:T(8,128)S(1)} %get-tuple-element.96) | copy-start | bytes 3145732
  140.6 11.5 %copy-start.36 = (f32[512,512]{1,0:T(8,128)S(1)}, f32[512,512]{1,0:T(8,128)}, u32[]{:S(2)}) copy-start(f32[512,512]{1,0:T(8,128)} %get-tuple-element.106) | copy-start | bytes 3145732
  140.6 11.5 %copy-start.58 = (bf16[2048,512]{1,0:T(8,128)(2,1)S(1)}, bf16[2048,512]{1,0:T(8,128)(2,1)}, u32[]{:S(2)}) copy-start(bf16[2048,512]{1,0:T(8,128)(2,1)} %param.36) | copy-start | bytes 6291460
  171.7 16.8 %copy-start.18 = (f32[128,1024]{1,0:T(8,128)S(1)}, f32[128,1024]{1,0:T(8,128)}, u32[]{:S(2)}) copy-start(f32[128,1024]{1,0:T(8,128)} %copy-done.17) | copy-start | bytes 1572868
  188.5 12.7 %copy-start.16 = (bf16[4,128,8,64]{1,3,2,0:T(8,128)(2,1)S(1)}, bf16[4,128,8,64]{1,3,2,0:T(8,128)(2,1)}, u32[]{:S(2)}) copy-start(bf16[4,128,8,64]{1,3,2,0:T(8,128)(2,1)} %copy-done.15) | copy-start | bytes 1572868
  212.2 99.2 %reduce-scatter.5.cloned.1.call-start = ((), (), s32[]{:S(2)}) async-start(), calls=%async_computation.5 | async-start | bytes 4718592 | tf_op jit(solution)/shard_map/reduce_scatter | solution.py:454
  266.5 49.0 %copy-start.45 = (f32[512]{0:T(512)S(1)}, f32[512]{0:T(512)}, u32[]{:S(2)}) copy-start(f32[512]{0:T(512)} %copy-done.44) | copy-start | bytes 6148
  266.5 49.0 %copy-start.47 = (f32[512]{0:T(512)S(1)}, f32[512]{0:T(512)}, u32[]{:S(2)}) copy-start(f32[512]{0:T(512)} %param.25) | copy-start | bytes 6148
  322.6 11.3 %copy-start.39 = (bf16[512,512]{1,0:T(8,128)(2,1)S(1)}, bf16[512,512]{1,0:T(8,128)(2,1)}, u32[]{:S(2)}) copy-start(bf16[512,512]{1,0:T(8,128)(2,1)} %convolution_convert_fusion.4) | copy-start | bytes 1572868
  322.6 14.0 %copy-start.23 = (bf16[512,2048]{1,0:T(8,128)(2,1)S(1)}, bf16[512,2048]{1,0:T(8,128)(2,1)}, u32[]{:S(2)}) copy-start(bf16[512,2048]{1,0:T(8,128)(2,1)} %convolution_convert_fusion.3) | copy-start | bytes 6291460
  325.9 21.8 %copy-start.26 = (bf16[2048,512]{1,0:T(8,128)(2,1)S(1)}, bf16[2048,512]{1,0:T(8,128)(2,1)}, u32[]{:S(2)}) copy-start(bf16[2048,512]{1,0:T(8,128)(2,1)} %convolution_convert_fusion.2) | copy-start | bytes 6291460
  336.6 14.5 %copy-start.35 = (bf16[512,1536]{1,0:T(8,128)(2,1)S(1)}, bf16[512,1536]{1,0:T(8,128)(2,1)}, u32[]{:S(2)}) copy-start(bf16[512,1536]{1,0:T(8,128)(2,1)} %convolution_convert_fusion) | copy-start | bytes 4718596
  458.9 9.2 %copy-start.50 = (f32[56,128]{1,0:T(8,128)S(1)}, f32[56,128]{1,0:T(8,128)}, u32[]{:S(2)}) copy-start(f32[56,128]{1,0:T(8,128)} %get-tuple-element.22) | copy-start | bytes 86020
  474.8 37.0 %collective-permute-start.1 = (f32[4,2,512]{2,1,0:T(2,128)S(1)}, f32[4,2,512]{2,1,0:T(2,128)S(1)}, u32[]{:S(2)}, u32[]{:S(2)}) collective-permute-start(f32[4,2,512]{2,1,0:T(2,128)S(1)} %slice.533), channel_id=1, source_target_pairs={{1,0},{2,1},{3,2},{4,3},{5,4},{6,5},{7,6},{9,8},{10,9},{11,10},{12... | collective-permute-start | bytes 49160 | tf_op jit(solution)/shard_map/ppermute | solution.py:304
  (53 other events, 222.7 us)
Sparse Core Ops, SparseCore 0:
  23.7 51.6 all-gather.4
  77.5 45.8 all-gather.2
  212.3 48.7 reduce-scatter.2
  263.2 48.1 reduce-scatter.4

commit v2 on v1

v2 whole, which is shorter than its diff:
```python
import functools
import math

import jax
import jax.numpy as jnp
from jax import lax
from jax.experimental import pallas as pl
from jax.experimental.pallas import tpu as pltpu
from jax.sharding import PartitionSpec as P

norm_eps = 1e-05
log2_e = math.log2(math.e)

MESH = pl.DeviceIdType.MESH
half = jnp.bfloat16
full = jnp.float32


class Place:
    def __init__(self, batch_size, seq_size):
        side = math.isqrt(batch_size)
        self.depth = seq_size // 2
        self.batch = lax.axis_index("batch")
        self.seq = lax.axis_index("seq")
        self.core = self.seq % 2
        self.level = self.seq // 2
        high, low = self.batch // side, self.batch % side
        self.first = jnp.where(self.core == 0, low, high)
        self.second = jnp.where(self.core == 0, high, low)
        self.side = side
        self.sizes = (2, side, side, self.depth)
        self.where = (self.core, self.first, self.second, self.level)

    def batch_at(self, first, second):
        return jnp.where(
            self.core == 0, second * self.side + first, first * self.side + second
        )

    def partner(self, stage, step):
        member = (self.where[stage] + step) % self.sizes[stage]
        if stage == 0:
            return (self.batch, self.level * 2 + member)
        if stage == 1:
            return (self.batch_at(member, self.second), self.seq)
        if stage == 2:
            return (self.batch_at(self.first, member), self.seq)
        return (self.batch, member * 2 + self.core)

    def partners(self):
        return [
            self.partner(stage, step)
            for stage in range(4)
            for step in range(1, self.sizes[stage])
        ]


def sum_slots(batch_size, seq_size):
    return 1 + 2 * (math.isqrt(batch_size) - 1) + seq_size // 2 - 1


class SumPieces:
    def __init__(self, place, chunks, mine, landing, piece, out, sems, keep):
        self.place, self.chunks = place, chunks
        self.mine, self.landing, self.piece, self.out = mine, landing, piece, out
        self.keep = keep
        self.sent, self.got, self.back_sent, self.back_got = sems
        self.starts = [sum(chunks[:c]) for c in range(len(chunks))]
        sizes = place.sizes
        self.slot = [sum(s - 1 for s in sizes[:stage]) for stage in range(4)]
        self.land = {}
        at = 0
        for c in range(len(chunks)):
            for stage in range(4):
                for step in range(1, sizes[stage]):
                    self.land[c, stage, step] = at
                    at += self.rows(c, stage)

    @staticmethod
    def landing_rows(batch_size, seq_size, chunks):
        side = math.isqrt(batch_size)
        rows, left = 0, sum(chunks)
        for size in (2, side, side, seq_size // 2):
            left //= size
            rows += left * (size - 1)
        return rows

    def rows(self, c, stage):
        count = self.chunks[c]
        for size in self.place.sizes[: stage + 1]:
            count //= size
        return count

    def begin(self, c, stage):
        at = self.starts[c]
        for t in range(stage):
            at = at + self.place.where[t] * self.rows(c, t)
        return at

    def scatter(self, c, stage, step):
        count = self.rows(c, stage)
        member = (self.place.where[stage] + step) % self.place.sizes[stage]
        at = pl.multiple_of(self.begin(c, stage) + member * count, 16)
        slot = self.slot[stage] + step - 1
        return pltpu.make_async_remote_copy(
            src_ref=self.mine.at[pl.ds(at, count), :],
            dst_ref=self.landing.at[pl.ds(self.land[c, stage, step], count), :],
            send_sem=self.sent.at[c, slot],
            recv_sem=self.got.at[c, slot],
            device_id=self.place.partner(stage, step),
            device_id_type=MESH,
        )

    def piece_span(self, c):
        return pl.ds(self.starts[c] * self.rows(c, 3) // self.chunks[c], self.rows(c, 3))

    def keep_copy(self, c):
        at = pl.multiple_of(self.begin(c, 4), 16)
        return pltpu.make_async_copy(
            self.piece.at[self.piece_span(c), :],
            self.out.at[pl.ds(at, self.rows(c, 3)), :],
            self.keep.at[c],
        )

    def gather(self, c, stage, step):
        count = self.rows(c, stage)
        at = pl.multiple_of(self.begin(c, stage + 1), 16)
        slot = self.slot[stage] + step - 1
        source = self.out.at[pl.ds(at, count), :]
        if stage == 3:
            source = self.piece.at[self.piece_span(c), :]
        return pltpu.make_async_remote_copy(
            src_ref=source,
            dst_ref=self.out.at[pl.ds(at, count), :],
            send_sem=self.back_sent.at[c, slot],
            recv_sem=self.back_got.at[c, slot],
            device_id=self.place.partner(stage, step),
            device_id_type=MESH,
        )

    def add(self, c, stage):
        count = self.rows(c, stage)
        at = self.begin(c, stage + 1)
        part = min(count, 128)

        def body(i, carry):
            here = pl.multiple_of(at + i * part, 16)
            total = self.mine[pl.ds(here, part), :].astype(full)
            for step in range(1, self.place.sizes[stage]):
                there = pl.multiple_of(self.land[c, stage, step] + i * part, 16)
                total = total + self.landing[pl.ds(there, part), :].astype(full)
            if stage == 3:
                first = self.piece_span(c).start
                self.piece[pl.ds(pl.multiple_of(first + i * part, 16), part), :] = total.astype(half)
            else:
                self.mine[pl.ds(here, part), :] = total.astype(half)
            return carry

        lax.fori_loop(0, count // part, body, 0)

    def steps(self, stage):
        return range(1, self.place.sizes[stage])

    def advance(self, c, event):
        if 1 <= event <= 4:
            for step in self.steps(event - 1):
                self.scatter(c, event - 1, step).wait_recv()
            self.add(c, event - 1)
        if event <= 3:
            for step in self.steps(event):
                self.scatter(c, event, step).start()
        else:
            stage = 7 - event
            if event == 4:
                self.keep_copy(c).start()
            else:
                for step in self.steps(stage + 1):
                    self.gather(c, stage + 1, step).wait_recv()
            if event == 5:
                self.keep_copy(c).wait()
            if event <= 7:
                for step in self.steps(stage):
                    self.gather(c, stage, step).start()

    def finish(self):
        for c in range(len(self.chunks)):
            for stage in range(4):
                for step in self.steps(stage):
                    self.scatter(c, stage, step).wait_send()
                    self.gather(c, stage, step).wait_send()


class SumSmall:
    def __init__(self, place, block, landing, sems):
        self.place, self.block, self.landing = place, block, landing
        self.sent, self.got = sems
        sizes = place.sizes
        self.slot = [sum(s - 1 for s in sizes[:stage]) for stage in range(4)]
        self.base = [sum(sizes[:stage]) for stage in range(4)]

    def copy(self, stage, step):
        slot = self.slot[stage] + step - 1
        return pltpu.make_async_remote_copy(
            src_ref=self.block.at[stage],
            dst_ref=self.landing.at[self.base[stage] + self.place.where[stage]],
            send_sem=self.sent.at[slot],
            recv_sem=self.got.at[slot],
            device_id=self.place.partner(stage, step),
            device_id_type=MESH,
        )

    def send(self, stage):
        self.landing[self.base[stage] + self.place.where[stage]] = self.block[stage]
        for step in range(1, self.place.sizes[stage]):
            self.copy(stage, step).start()

    def receive(self, stage):
        for step in range(1, self.place.sizes[stage]):
            self.copy(stage, step).wait_recv()
        total = self.landing[self.base[stage]]
        for member in range(1, self.place.sizes[stage]):
            total = total + self.landing[self.base[stage] + member]
        self.block[stage + 1] = total

    def finish(self):
        for stage in range(4):
            for step in range(1, self.place.sizes[stage]):
                self.copy(stage, step).wait_send()


def dot_nn(left, right):
    return lax.dot_general(
        left, right, (((1,), (0,)), ((), ())), preferred_element_type=full
    )


def dot_nt(left, right):
    return lax.dot_general(
        left, right, (((1,), (1,)), ((), ())), preferred_element_type=full
    )


def dot_tn(left, right):
    return lax.dot_general(
        left, right, (((0,), (0,)), ((), ())), preferred_element_type=full
    )


def centred_rows(values_in):
    centre = values_in - jnp.mean(values_in, axis=-1, keepdims=True)
    spread = jnp.mean(centre * centre, axis=-1, keepdims=True)
    inverse = lax.rsqrt(spread + norm_eps)
    return centre * inverse, inverse


def norm_back(grad_normed, scaled, inverse, gain):
    inner = grad_normed * gain
    first = jnp.mean(inner, axis=-1, keepdims=True)
    second = jnp.mean(inner * scaled, axis=-1, keepdims=True)
    return inverse * (inner - first - scaled * second)


class Sizes:
    def __init__(self, batch_size, seq_size, rows, block, width, hidden, heads):
        self.batch, self.seq = batch_size, seq_size
        self.rows, self.block, self.width, self.hidden = rows, block, width, hidden
        self.heads = heads
        self.tokens = rows * block
        self.length = seq_size * block
        self.depth = seq_size // 2
        self.per_row = seq_size // rows
        self.chips_per_row = self.per_row // 2
        self.own_width = width // self.per_row
        self.own_heads = heads // self.per_row
        self.pairs = self.own_heads // 2
        self.head_dim = width // heads
        self.span = 2 * block
        self.query_blocks = self.length // self.span
        self.reach = self.query_blocks // 2
        self.tiles = []
        for i in range(self.query_blocks):
            for j in range(max(0, i - self.reach), i + 1):
                self.tiles.append((i, j))
        self.lanes = width // 128
        self.parts = hidden // width


def product_list(parts):
    order = []
    for j in range(parts):
        order += [("inner", j), ("outer", j)]
    order += [("up", 0), ("up", 1), ("up", 2), ("out", 0)]
    order += [("query", 0), ("key", 0), ("value", 0)]
    order += [("pool", 0), ("pool", 1), ("pool", 2)]
    return order


small_places = (
    ("pool_bias", 0), ("gain_one", 4), ("shift_one", 8), ("slopes", 12),
    ("gain_two", 13), ("shift_two", 17), ("inner_bias", 21), ("outer_bias", 37),
    ("up_bias", 41),
)
small_rows = 56


def layer_kernel(size, chunks, lag, docs, slopes, pool_bias, gain_one, shift_one,
                 gain_two, shift_two, inner_bias, outer_bias, up_bias,
                 inputs_hbm, cotangent_hbm, pool_hbm, query_hbm, key_hbm, value_hbm,
                 out_hbm, inner_hbm, outer_hbm, up_hbm,
                 output_hbm, shift_hbm, sums_hbm, small_out,
                 *scratch_refs):
    names = [name for name, _ in scratch_plan(size, chunks)]
    s = dict(zip(names, scratch_refs))
    place = Place(size.batch, size.seq)
    me, core, level = place.seq, place.core, place.level
    rows, block, width, hidden = size.rows, size.block, size.width, size.hidden
    tokens, length, depth = size.tokens, size.length, size.depth
    per_row, chips = size.per_row, size.chips_per_row
    own_width, pairs = size.own_width, size.pairs
    my_row, my_group = me // per_row, me % per_row
    lanes, parts, span = size.lanes, size.parts, size.span
    products = product_list(parts)
    product_rows = width * lanes

    def tile_at(name, part, lane):
        return products.index((name, part)) * product_rows + lane * width

    loads = {}

    def load(name, source, target):
        copy = pltpu.make_async_copy(source, target, s["load_sem"].at[len(loads)])
        copy.start()
        loads[name] = copy

    first_column = pl.multiple_of(my_group * own_width, own_width)

    def x_load(step):
        return pltpu.make_async_copy(
            inputs_hbm.at[(my_row + 1 + step) % rows], s["x"].at[step % 2],
            s["x_sem"].at[step % 2],
        )

    x_load(0).start()
    load("pool", pool_hbm, s["pool_w"])
    load("dy", cotangent_hbm, s["raised"])
    load("up", up_hbm, s["up_w"])
    load("query", query_hbm.at[:, pl.ds(first_column, own_width)], s["query_w"])
    load("key", key_hbm.at[:, pl.ds(first_column, own_width)], s["key_w"])
    load("value", value_hbm.at[:, pl.ds(first_column, own_width)], s["value_w"])
    load("outer", outer_hbm, s["outer_w"])
    load("out", out_hbm, s["out_w"])
    load("inner", inner_hbm, s["inner_w"])

    barrier = pltpu.get_barrier_semaphore()
    greeted = [(place.batch, (me + k) % size.seq) for k in range(1, size.seq)]
    for stage in (1, 2):
        greeted += [place.partner(stage, k) for k in range(1, place.sizes[stage])]
    for device in greeted:
        pl.semaphore_signal(barrier, inc=1, device_id=device, device_id_type=MESH)
    pl.semaphore_wait(barrier, len(greeted))

    def remote(source, target, sent, got, device):
        return pltpu.make_async_remote_copy(
            src_ref=source, dst_ref=target, send_sem=sent, recv_sem=got,
            device_id=device, device_id_type=MESH,
        )

    rim_copy = remote(
        inputs_hbm.at[:, pl.ds(3 * block - 16, 16), :], s["rim"],
        s["rim_sem"].at[0], s["rim_sem"].at[1], (place.batch, (me + 1) % size.seq),
    )

    @pl.when(me < size.seq - 1)
    def _():
        rim_copy.start()

    small_block = s["small_block"]
    small_block[0] = jnp.zeros((small_rows, 128), full)
    small_at = dict(small_places)

    def put_small(name, at, values):
        for c in range(values.shape[1] // 128):
            small_block[0, pl.ds(small_at[name] + at // 128 + c, 1), :] = values[
                :, c * 128 : (c + 1) * 128
            ]

    stage = s["stage"]

    def spread_rows(at, values):
        for c in range(lanes):
            stage[c, pl.ds(at, values.shape[0]), :] = values[:, c * 128 : (c + 1) * 128]

    def every_third(at):
        return jnp.concatenate(
            [stage[c, pl.ds(at, block, stride=3), :] for c in range(lanes)], axis=1
        )

    def put_third(at, values):
        for c in range(lanes):
            stage[c, pl.ds(at, block, stride=3), :] = values[:, c * 128 : (c + 1) * 128]

    def row_span(r):
        return pl.ds(pl.multiple_of(r * block, block), block)

    loads["dy"].wait()
    loads["up"].wait()
    up_sum = jnp.zeros((1, width), full)

    def split_cotangent(r, carry):
        spread_rows(8, s["raised"][r].astype(full))
        totals = []
        grad = jnp.zeros((block, width), full)
        for k in range(3):
            part = every_third(8 + k)
            totals.append(carry[k] + jnp.sum(part, axis=0, keepdims=True))
            low = part.astype(half)
            s["dy"][row_span(r), k * width : (k + 1) * width] = low
            grad = grad + dot_nt(low, s["up_w"][:, k * width : (k + 1) * width])
        s["grad_resid"][row_span(r), :] = grad
        low = grad.astype(half)
        s["grad_branch"][row_span(r), :] = low
        totals.append(carry[3] + jnp.sum(low.astype(full), axis=0, keepdims=True))
        return tuple(totals)

    sums = lax.fori_loop(0, rows, split_cotangent, (up_sum,) * 4)
    load("x", inputs_hbm, s["raised"])
    for k in range(3):
        put_small("up_bias", k * width, sums[k])
    put_small("outer_bias", 0, sums[3])

    @pl.when(me > 0)
    def _():
        rim_copy.wait_recv()

    loads["pool"].wait()
    nr = s["nr"]

    def nr_rows(owner):
        return pl.ds(pl.multiple_of(owner * block, block), block)

    def row_copy(r, target_level):
        return remote(
            s["normed"].at[row_span(r), :], nr.at[nr_rows(me), :],
            s["row_sent"].at[target_level], s["row_got"].at[level],
            (place.batch, target_level * 2 + core),
        )

    def row_from(source_level):
        return remote(
            s["normed"].at[row_span(0), :], nr.at[nr_rows(source_level * 2 + core), :],
            s["row_sent"].at[source_level], s["row_got"].at[source_level],
            (place.batch, source_level * 2 + core),
        )

    for step in range(rows):
        r = (my_row + 1 + step) % rows
        rim_rows = s["rim"][r].astype(full)[8:16, :]
        rim_rows = jnp.where(me > 0, rim_rows, 0.0)
        spread_rows(0, rim_rows)
        x_load(step).wait()
        if step + 1 < rows:
            x_load(step + 1).start()
        spread_rows(8, s["x"][step % 2].astype(full))
        pooled = jnp.zeros((block, width), full) + pool_bias[...]
        for k in range(3):
            part = every_third(6 + k).astype(half)
            s["groups"][row_span(r), k * width : (k + 1) * width] = part
            pooled = pooled + dot_nn(part, s["pool_w"][k * width : (k + 1) * width, :])
        s["pooled"][row_span(r), :] = pooled
        scaled, _ = centred_rows(pooled)
        s["normed"][row_span(r), :] = (scaled * gain_one[...] + shift_one[...]).astype(half)
        if step < rows - 1:
            for i in range(chips):
                row_copy(r, r * chips + i).start()
        else:
            for i in range(1, chips):
                row_copy(r, r * chips + (level % chips + i) % chips).start()
            own_copy = pltpu.make_async_copy(
                s["normed"].at[row_span(r), :], nr.at[nr_rows(me), :], s["own_sem"].at[0]
            )
            own_copy.start()

    loads["outer"].wait()

    def before_activation(j, carry):
        at = pl.ds(pl.multiple_of(j * width, width), width)
        grad = dot_nt(s["grad_branch"][...], s["outer_w"][at, :])
        s["grad_inner"][:, at] = grad.astype(half)
        return carry

    lax.fori_loop(0, parts, before_activation, 0)

    def across(source_level, owner_core):
        owner = source_level * 2 + owner_core
        return remote(
            nr.at[nr_rows(owner), :], nr.at[nr_rows(owner), :],
            s["across_sent"].at[source_level], s["across_got"].at[source_level],
            (place.batch, level * 2 + 1 - core),
        )

    loads["query"].wait()
    loads["key"].wait()
    loads["value"].wait()

    def project(owner):
        at = nr_rows(owner)
        source = nr[at, :]
        q = dot_nn(source, s["query_w"][...])
        k = dot_nn(source, s["key_w"][...])
        v = dot_nn(source, s["value_w"][...])
        qt, kt, vt = q.T, k.T, v.T
        s["vt"][:, at] = vt.astype(half)
        zeros = jnp.zeros((64, block), half)
        line = lax.broadcasted_iota(jnp.int32, (16, block), 0)
        key_at = owner * block + lax.broadcasted_iota(jnp.int32, (16, block), 1)
        fine = (key_at % 128).astype(full)
        coarse = (key_at - key_at % 128).astype(full)
        extra = jnp.where(line == 0, 1.0, jnp.where(line == 1, fine, coarse))
        extra = jnp.where(line < 3, extra, 0.0).astype(half)
        for p in range(pairs):
            s["k"][p, at, :] = k[:, p * 128 : (p + 1) * 128].astype(half)
            s["v"][p, at, :] = v[:, p * 128 : (p + 1) * 128].astype(half)
            for side in range(2):
                h = 2 * p + side
                piece = qt[h * 64 : (h + 1) * 64, :].astype(half)
                s["qt"][h, :, at] = jnp.concatenate(
                    [piece, zeros] if side == 0 else [zeros, piece], axis=0
                )
                piece = kt[h * 64 : (h + 1) * 64, :].astype(half)
                s["kt"][h, :, at] = jnp.concatenate([piece, extra], axis=0)

    order = [0]
    for k in range(1, depth):
        order.append((k + 1) // 2 if k % 2 else depth - k // 2)
    for k in order:
        source_level = (level + k) % depth
        if k == 0:
            own_copy.wait()
        else:
            row_from(source_level).wait_recv()
        across(source_level, core).start()
    for k in order:
        source_level = (level + k) % depth
        project(source_level * 2 + core)
        across(source_level, 1 - core).wait_recv()
        project(source_level * 2 + 1 - core)

    ends = []
    total = 0
    for d in range(docs.shape[1]):
        total = total + docs[my_row, d]
        ends.append(total)
    key_line = lax.broadcasted_iota(jnp.int32, (span, span), 0)
    query_line = lax.broadcasted_iota(jnp.int32, (span, span), 1)
    scale_two = size.head_dim ** -0.5 * log2_e

    def tile_of(i, j):
        return size.tiles.index((i, j))

    def near(i):
        return range(max(0, i - size.reach), i + 1)

    def att_copy(owner, at_row, at_group, slot):
        return remote(
            s["att_out"].at[nr_rows(owner), :],
            s["att"].at[row_span(at_row), pl.ds(pl.multiple_of(at_group * own_width, own_width), own_width)],
            s["att_sent"].at[owner], s["att_got"].at[slot], (place.batch, owner),
        )

    def head_slope(h):
        return slopes[my_group * size.own_heads + h]

    for i in range(size.query_blocks):
        cols = slice(i * span, (i + 1) * span)
        place_q = 3 * (i * span + lax.broadcasted_iota(jnp.int32, (1, span), 1))
        start = jnp.zeros((1, span), jnp.int32)
        for end in ends:
            start = jnp.where(end <= place_q, jnp.maximum(start, end), start)
        for w, j in enumerate(near(i)):
            allowed = 3 * (j * span + key_line) >= start
            if j == i:
                allowed = allowed & (key_line <= query_line)
            s["work"][size.reach + 1 + w] = jnp.where(allowed, 0.0, -1e30)

        def forward_pair(p, carry):
            for side in range(2):
                h = 2 * p + side
                slope_two = head_slope(h) * log2_e
                top = None
                for w, j in enumerate(near(i)):
                    score = dot_nn(s["k"][p, j * span : (j + 1) * span, :], s["qt"][h, :, cols])
                    away = (key_line + (j - i) * span).astype(full)
                    score = score * scale_two + (away * slope_two + s["work"][size.reach + 1 + w])
                    s["work"][w] = score
                    best = jnp.max(score, axis=0, keepdims=True)
                    top = best if top is None else jnp.maximum(top, best)
                total = jnp.zeros((1, span), full)
                mixed = jnp.zeros((64, span), full)
                for w, j in enumerate(near(i)):
                    expo = jnp.exp2(s["work"][w] - top)
                    total = total + jnp.sum(expo, axis=0, keepdims=True)
                    low = expo.astype(half)
                    s["expo"][h, tile_of(i, j)] = low
                    at = pl.multiple_of(h * 64, 64)
                    mixed = mixed + dot_nn(
                        s["vt"][pl.ds(at, 64), j * span : (j + 1) * span], low
                    )
                inverse = 1.0 / total
                s["inverse"][h, :, cols] = jnp.broadcast_to(inverse, (8, span))
                s["mixed"][pl.ds(pl.multiple_of(h * 64, 64), 64), cols] = mixed * inverse
            return carry

        lax.fori_loop(0, pairs, forward_pair, 0)
        s["att_out"][cols, :] = s["mixed"][:, cols].T.astype(half)
        for owner in (2 * i, 2 * i + 1):

            @pl.when(me == owner)
            def _():
                copy = pltpu.make_async_copy(
                    s["att_out"].at[nr_rows(owner), :],
                    s["att"].at[row_span(my_row), pl.ds(first_column, own_width)],
                    s["own_sem"].at[1],
                )
                copy.start()

            @pl.when(me != owner)
            def _():
                att_copy(owner, my_row, my_group, me).start()

    loads["out"].wait()
    loads["inner"].wait()
    pltpu.make_async_copy(
        s["att_out"].at[nr_rows(0), :],
        s["att"].at[row_span(my_row), pl.ds(first_column, own_width)],
        s["own_sem"].at[1],
    ).wait()
    for k in range(1, size.seq):
        source = (me + k) % size.seq
        att_copy(source, source // per_row, source % per_row, source).wait_recv()

    def second_norm(r, carry):
        at = row_span(r)
        residual = s["pooled"][at, :] + dot_nn(s["att"][at, :], s["out_w"][...])
        s["residual"][at, :] = residual
        scaled, _ = centred_rows(residual)
        s["normed_two"][at, :] = (scaled * gain_two[...] + shift_two[...]).astype(half)
        return carry

    lax.fori_loop(0, rows, second_norm, 0)

    for j in range(parts):
        at = slice(j * width, (j + 1) * width)

        def feed(r, carry):
            here = row_span(r)
            value = dot_nn(s["normed_two"][here, :], s["inner_w"][:, at]) + inner_bias[:, at]
            share = 0.5 + 0.5 * lax.erf(value * (0.5 ** 0.5))
            density = jnp.exp(-0.5 * value * value) * (0.5 / math.pi) ** 0.5
            s["activated"][here, at] = (value * share).astype(half)
            grad = s["grad_inner"][here, at].astype(full) * (share + value * density)
            low = grad.astype(half)
            s["grad_inner"][here, at] = low
            return carry + jnp.sum(low.astype(full), axis=0, keepdims=True)

        total = lax.fori_loop(0, rows, feed, jnp.zeros((1, width), full))
        put_small("inner_bias", j * width, total)

    def grad_copy(owner, slot):
        row, group = owner // per_row, owner % per_row
        column = pl.ds(pl.multiple_of(group * own_width, own_width), own_width)
        return remote(
            s["grad_att"].at[row_span(row), column], s["grad_heads"].at[nr_rows(slot), :],
            s["grad_sent"].at[owner], s["grad_got"].at[slot], (place.batch, owner),
        )

    gain_sum = jnp.zeros((1, width), full)
    shift_sum = jnp.zeros((1, width), full)
    for step in range(rows):
        r = (my_row + 1 + step) % rows
        at = row_span(r)
        grad = dot_nt(s["grad_inner"][at, :], s["inner_w"][...])
        scaled, inverse = centred_rows(s["residual"][at, :])
        gain_sum = gain_sum + jnp.sum(grad * scaled, axis=0, keepdims=True)
        shift_sum = shift_sum + jnp.sum(grad, axis=0, keepdims=True)
        mixed = s["grad_resid"][at, :] + norm_back(grad, scaled, inverse, gain_two[...])
        s["grad_resid"][at, :] = mixed
        s["grad_att"][at, :] = dot_nt(mixed.astype(half), s["out_w"][...]).astype(half)
        for g in range(per_row):
            owner = r * per_row + g
            if step < rows - 1:
                grad_copy(owner, me).start()
            else:

                @pl.when(owner != me)
                def _():
                    grad_copy(owner, me).start()

                @pl.when(owner == me)
                def _():
                    pltpu.make_async_copy(
                        s["grad_att"].at[row_span(my_row), pl.ds(first_column, own_width)],
                        s["grad_heads"].at[nr_rows(me), :], s["own_sem"].at[2],
                    ).start()
    put_small("gain_two", 0, gain_sum)
    put_small("shift_two", 0, shift_sum)

    big = SumPieces(place, chunks, s["mine"], s["landing"], s["piece"], sums_hbm,
                    [s["sum_sem"].at[k] for k in range(4)], s["keep_sem"])
    clock = [0]
    begun = {}

    def tick():
        for c in sorted(begun):
            event, off = divmod(clock[0] - begun[c], lag)
            if off == 0 and 0 <= event <= 8:
                big.advance(c, event)
        clock[0] += 1

    def begin(c):
        begun[c] = clock[0]

    def put_product(at, value):
        for c in range(value.shape[1] // 128):
            s["mine"][pl.ds(at + c * width, width), :] = value[
                :, c * 128 : (c + 1) * 128
            ].astype(half)

    for j in range(parts):
        at = slice(j * width, (j + 1) * width)
        put_product(tile_at("inner", j, 0), dot_tn(s["normed_two"][...], s["grad_inner"][:, at]))
        put_product(tile_at("outer", j, 0), dot_tn(s["activated"][:, at], s["grad_branch"][...]))
        begin(j)
        tick()

    def second_residual(r, carry):
        at = row_span(r)
        value = s["residual"][at, :] + dot_nn(s["activated"][at, :], s["outer_w"][...])
        s["normed_two"][at, :] = (value + outer_bias[...]).astype(half)
        return carry

    lax.fori_loop(0, rows, second_residual, 0)
    for k in range(3):
        at = slice(k * width, (k + 1) * width)
        put_product(tile_at("up", k, 0), dot_tn(s["normed_two"][...], s["dy"][:, at]))
        if k == 1:
            begin(parts)
            tick()
    put_product(tile_at("out", 0, 0), dot_tn(s["att"][...], s["grad_resid"][...].astype(half)))
    begin(parts + 1)
    tick()

    def raise_row(r, carry):
        for k in range(3):
            at = slice(k * width, (k + 1) * width)
            raised = dot_nn(s["normed_two"][row_span(r), :], s["up_w"][:, at])
            put_third(8 + k, raised + up_bias[:, at])
        whole = jnp.concatenate([stage[c, 8 : 8 + 3 * block, :] for c in range(lanes)], axis=1)
        s["raised"][r] = (s["raised"][r].astype(full) + whole).astype(half)
        return carry

    loads["x"].wait()
    lax.fori_loop(0, rows, raise_row, 0)
    output_copy = pltpu.make_async_copy(s["raised"], output_hbm, s["own_sem"].at[3])
    output_copy.start()

    blank = jnp.zeros((width, 128), half)
    for name in ("query", "key", "value"):
        for c in range(lanes):
            s["mine"][pl.ds(tile_at(name, 0, c), width), :] = blank

    pltpu.make_async_copy(
        s["grad_att"].at[row_span(my_row), pl.ds(first_column, own_width)],
        s["grad_heads"].at[nr_rows(me), :], s["own_sem"].at[2],
    ).wait()
    for k in range(1, size.seq):
        grad_copy((me + k) % size.seq, (me + k) % size.seq).wait_recv()

    half_blocks = size.query_blocks // 2

    def value_tile(p, j):
        lane = pl.multiple_of((p * half_blocks + j // 2) * 128, 128)
        return s["residual"].at[(j % 2) * span : (j % 2 + 1) * span, pl.ds(lane, 128)]

    def value_block(p, b):
        lane = pl.multiple_of((p * half_blocks + b // 4) * 128, 128)
        return s["residual"].at[row_span(b % 4), pl.ds(lane, 128)]

    def key_tile(p, j):
        at = p * half_blocks + j // 2
        return s["work"].at[at, :, (j % 2) * 128 : (j % 2 + 1) * 128]

    def key_block(p, b):
        lane = pl.multiple_of(b // 2 % 2 * 128, 128)
        return s["work"].at[p * half_blocks + b // 4, row_span(b % 2), pl.ds(lane, 128)]

    turned = s["work"].at[2 * size.reach + 1, 0:own_width, :]

    for i in range(size.query_blocks):
        cols = slice(i * span, (i + 1) * span)
        turned[...] = s["grad_heads"][cols, :].astype(full).T
        query_at = (i * span + lax.broadcasted_iota(jnp.int32, (1, span), 1)).astype(full)

        def backward_pair(p, carry):
            for side in range(2):
                h = 2 * p + side
                head = pl.ds(pl.multiple_of(h * 64, 64), 64)
                inverse = s["inverse"][h, 0:1, cols]
                grad = turned[head, :] * inverse
                term = jnp.sum(grad * s["mixed"][head, cols], axis=0, keepdims=True)
                low = grad.astype(half)
                zeros = jnp.zeros((64, span), half)
                low = jnp.concatenate([low, zeros] if side == 0 else [zeros, low], axis=0)
                query_grad = jnp.zeros((80, span), full)
                for j in near(i):
                    keys = slice(j * span, (j + 1) * span)
                    expo = s["expo"][h, tile_of(i, j)]
                    grad_probs = dot_nn(s["v"][p, keys, :], low)
                    grad_scores = (expo.astype(full) * (grad_probs - term)).astype(half)
                    to_value = dot_nt(expo, low)
                    to_key = dot_nt(grad_scores, s["qt"][h, :, cols])
                    if j == i and side == 0:
                        value_tile(p, j)[...] = to_value
                        key_tile(p, j)[...] = to_key
                    else:
                        value_tile(p, j)[...] += to_value
                        key_tile(p, j)[...] += to_key
                    query_grad = query_grad + dot_nn(s["kt"][h, :, keys], grad_scores)
                s["mixed"][head, cols] = query_grad[:64, :]
                slope = (
                    query_grad[65:66, :] + query_grad[66:67, :] - query_at * query_grad[64:65, :]
                )
                slope = jnp.broadcast_to(slope, (8, span))
                if i == 0:
                    s["slope_sum"][h] = slope
                else:
                    s["slope_sum"][h] += slope
            return carry

        lax.fori_loop(0, pairs, backward_pair, 0)
        tick()

    head_lane = lax.broadcasted_iota(jnp.int32, (1, 128), 1)
    slope_row = jnp.zeros((1, 128), full)
    for h in range(size.own_heads):
        total = jnp.sum(s["slope_sum"][h][0:1, :], axis=1, keepdims=True)
        slope_row = slope_row + jnp.where(head_lane == my_group * size.own_heads + h, total, 0.0)
    small_block[0, pl.ds(small_at["slopes"], 1), :] = slope_row

    scale = size.head_dim ** -0.5

    fit = width // own_width

    def grads_at(which, at=None):
        down = which // fit * length
        if at is None:
            at = pl.ds(down, length)
        else:
            at = pl.ds(pl.multiple_of(at + down, block), block)
        return s["outer_w"].at[at, which % fit * own_width : (which % fit + 1) * own_width]

    def settle(b, carry):
        at = nr_rows(b)
        for which in range(3):
            target = grads_at(which, b * block)
            if which == 0:
                target[...] = (s["mixed"][:, at].T * scale).astype(half)
                continue
            for p in range(pairs):
                lane = slice(p * 128, (p + 1) * 128)
                if which == 1:
                    target[:, lane] = (key_block(p, b)[...] * scale).astype(half)
                else:
                    target[:, lane] = value_block(p, b)[...].astype(half)
        return carry

    lax.fori_loop(0, size.seq, settle, 0)

    def normed_grad(owner):
        return (
            dot_nt(grads_at(0, owner * block)[...], s["query_w"][...])
            + dot_nt(grads_at(1, owner * block)[...], s["key_w"][...])
            + dot_nt(grads_at(2, owner * block)[...], s["value_w"][...])
        )

    def held(first, owner_level):
        across_at = (first + owner_level // rows) * width
        return s["activated"].at[
            row_span(owner_level % rows), pl.ds(pl.multiple_of(across_at, width), width)
        ]

    held_parts = -(-depth // rows)

    def pair_copy(owner_level):
        return remote(
            held(0, owner_level), s["pair_in"].at[row_span(owner_level), :],
            s["pair_sent"].at[owner_level], s["pair_got"].at[owner_level],
            (place.batch, level * 2 + 1 - core),
        )

    def back_copy(owner_level, source_level):
        row, part = source_level // chips, source_level % chips
        return remote(
            held(held_parts, owner_level),
            s["back"].at[part, row_span(row), :],
            s["back_sent"].at[owner_level], s["back_got"].at[source_level],
            (place.batch, owner_level * 2 + core),
        )

    for k in range(depth):
        owner_level = (level + 1 + k) % depth
        held(0, owner_level)[...] = normed_grad(owner_level * 2 + 1 - core).astype(half)
        pair_copy(owner_level).start()
    for k in range(depth):
        owner_level = (level + 1 + k) % depth
        grad = normed_grad(owner_level * 2 + core)
        pair_copy(owner_level).wait_recv()
        grad = grad + s["pair_in"][row_span(owner_level), :].astype(full)
        held(held_parts, owner_level)[...] = grad.astype(half)
        if k < depth - 1:
            back_copy(owner_level, level).start()
        else:
            back_own = pltpu.make_async_copy(
                held(held_parts, level),
                s["back"].at[level % chips, row_span(level // chips), :],
                s["own_sem"].at[4],
            )
            back_own.start()
    tick()

    for which, name in enumerate(("query", "key", "value")):
        value = dot_tn(nr[...], grads_at(which)[...])
        base = products.index((name, 0)) * product_rows
        for c in range(own_width // 128):
            at = pl.multiple_of(base + (my_group * (own_width // 128) + c) * width, width)
            s["mine"][pl.ds(at, width), :] = value[:, c * 128 : (c + 1) * 128].astype(half)
        if name == "key":
            begin(parts + 2)
            tick()

    back_own.wait()
    for k in range(1, depth):
        source_level = (level + k) % depth
        back_copy(source_level, source_level).wait_recv()

    def first_norm(r, carry):
        at = row_span(r)
        grad = s["back"][0, at, :].astype(full)
        for part in range(1, chips):
            grad = grad + s["back"][part, at, :].astype(full)
        scaled, inverse = centred_rows(s["pooled"][at, :])
        low = s["grad_resid"][at, :] + norm_back(grad, scaled, inverse, gain_one[...])
        low = low.astype(half)
        s["normed"][at, :] = low
        for k in range(3):
            put_third(6 + k, dot_nt(low, s["pool_w"][k * width : (k + 1) * width, :]))
        for c in range(lanes):
            lane = slice(c * 128, (c + 1) * 128)
            s["edge_out"][r, :, lane] = stage[c, 0:8, :]
            s["edge_end"][r, :, lane] = stage[c, 3 * block - 8 : 3 * block + 8, :]
            s["raised"][r, :, lane] = stage[c, 8 : 8 + 3 * block, :].astype(half)
        return (
            carry[0] + jnp.sum(grad * scaled, axis=0, keepdims=True),
            carry[1] + jnp.sum(grad, axis=0, keepdims=True),
            carry[2] + jnp.sum(low.astype(full), axis=0, keepdims=True),
        )

    output_copy.wait()
    for k in range(1, depth):
        row_from((level + k) % depth).wait_send()
    nothing = jnp.zeros((1, width), full)
    totals = lax.fori_loop(0, rows, first_norm, (nothing,) * 3)
    put_small("gain_one", 0, totals[0])
    put_small("shift_one", 0, totals[1])
    put_small("pool_bias", 0, totals[2])
    edge_copy = remote(
        s["edge_out"], s["edge_in"], s["rim_sem"].at[2], s["rim_sem"].at[3],
        (place.batch, (me + size.seq - 1) % size.seq),
    )

    @pl.when(me > 0)
    def _():
        edge_copy.start()

    small = SumSmall(place, small_block, s["small_landing"],
                     [s["small_sem"].at[0], s["small_sem"].at[1]])
    small.send(0)
    for k in range(3):
        at = slice(k * width, (k + 1) * width)
        put_product(tile_at("pool", k, 0), dot_tn(s["groups"][:, at], s["normed"][...]))
        if k == 0:
            begin(parts + 3)
            tick()
    begin(parts + 4)
    tick()
    small.receive(0)
    small.send(1)

    @pl.when(me < size.seq - 1)
    def _():
        edge_copy.wait_recv()

    edge_row = lax.broadcasted_iota(jnp.int32, (16, width), 0)
    for r in range(rows):
        edge = jnp.where(me < size.seq - 1, s["edge_in"][r], 0.0)
        edge = jnp.concatenate([edge, edge], axis=0)
        edge = jnp.where(edge_row >= 14, edge, s["edge_end"][r])
        s["raised"][r, 3 * block - 16 : 3 * block, :] = edge.astype(half)
    shift_copy = pltpu.make_async_copy(s["raised"], shift_hbm, s["own_sem"].at[5])
    shift_copy.start()

    stages_done = 1
    last = begun[parts + 4] + 8 * lag
    while clock[0] <= last:
        tick()
        if stages_done < 4 and clock[0] % 2 == 0:
            small.receive(stages_done)
            stages_done += 1
            if stages_done < 4:
                small.send(stages_done)
    while stages_done < 4:
        small.receive(stages_done)
        stages_done += 1
        if stages_done < 4:
            small.send(stages_done)
    small_out[...] = small_block[4]

    shift_copy.wait()

    @pl.when(me < size.seq - 1)
    def _():
        rim_copy.wait_send()

    @pl.when(me > 0)
    def _():
        edge_copy.wait_send()

    for k in range(1, depth):
        other = (level + k) % depth
        back_copy(other, other).wait_send()
    for k in range(depth):
        across(k, core).wait_send()
        pair_copy(k).wait_send()
    for k in range(1, size.seq):
        other = (me + k) % size.seq
        att_copy(other, other // per_row, other % per_row, other).wait_send()
        grad_copy(other, other).wait_send()
    big.finish()
    small.finish()


def scratch_plan(size, chunks):
    tokens, length, width, hidden = size.tokens, size.length, size.width, size.hidden
    rows, block, depth = size.rows, size.block, size.depth
    own, pairs, heads = size.own_width, size.pairs, size.own_heads
    near = size.reach + 1
    members = 2 + 2 * math.isqrt(size.batch) + depth
    slots = sum_slots(size.batch, size.seq)
    dma = pltpu.SemaphoreType.DMA
    total = sum(chunks)
    return [
        ("x", pltpu.VMEM((2, 3 * block, width), half)),
        ("raised", pltpu.VMEM((rows, 3 * block, width), half)),
        ("pool_w", pltpu.VMEM((3 * width, width), half)),
        ("up_w", pltpu.VMEM((width, 3 * width), half)),
        ("query_w", pltpu.VMEM((width, own), half)),
        ("key_w", pltpu.VMEM((width, own), half)),
        ("value_w", pltpu.VMEM((width, own), half)),
        ("outer_w", pltpu.VMEM((hidden, width), half)),
        ("inner_w", pltpu.VMEM((width, hidden), half)),
        ("out_w", pltpu.VMEM((width, width), half)),
        ("rim", pltpu.VMEM((rows, 16, width), half)),
        ("stage", pltpu.VMEM((size.lanes, 3 * block + 8, 128), full)),
        ("groups", pltpu.VMEM((tokens, 3 * width), half)),
        ("dy", pltpu.VMEM((tokens, 3 * width), half)),
        ("grad_resid", pltpu.VMEM((tokens, width), full)),
        ("grad_branch", pltpu.VMEM((tokens, width), half)),
        ("pooled", pltpu.VMEM((tokens, width), full)),
        ("normed", pltpu.VMEM((tokens, width), half)),
        ("nr", pltpu.VMEM((length, width), half)),
        ("grad_inner", pltpu.VMEM((tokens, hidden), half)),
        ("activated", pltpu.VMEM((tokens, hidden), half)),
        ("qt", pltpu.VMEM((heads, 128, length), half)),
        ("kt", pltpu.VMEM((heads, 80, length), half)),
        ("vt", pltpu.VMEM((own, length), half)),
        ("k", pltpu.VMEM((pairs, length, 128), half)),
        ("v", pltpu.VMEM((pairs, length, 128), half)),
        ("work", pltpu.VMEM((2 * near, size.span, size.span), full)),
        ("expo", pltpu.VMEM((heads, len(size.tiles), size.span, size.span), half)),
        ("inverse", pltpu.VMEM((heads, 8, length), full)),
        ("mixed", pltpu.VMEM((own, length), full)),
        ("att_out", pltpu.VMEM((length, own), half)),
        ("att", pltpu.VMEM((tokens, width), half)),
        ("residual", pltpu.VMEM((tokens, width), full)),
        ("normed_two", pltpu.VMEM((tokens, width), half)),
        ("grad_att", pltpu.VMEM((tokens, width), half)),
        ("grad_heads", pltpu.VMEM((length, own), half)),
        ("slope_sum", pltpu.VMEM((heads, 8, size.span), full)),
        ("pair_in", pltpu.VMEM((depth * block, width), half)),
        ("back", pltpu.VMEM((size.chips_per_row, tokens, width), half)),
        ("edge_out", pltpu.VMEM((rows, 8, width), full)),
        ("edge_in", pltpu.VMEM((rows, 8, width), full)),
        ("edge_end", pltpu.VMEM((rows, 16, width), full)),
        ("mine", pltpu.VMEM((total, 128), half)),
        ("landing", pltpu.VMEM((SumPieces.landing_rows(size.batch, size.seq, chunks), 128), half)),
        ("piece", pltpu.VMEM((total // (size.batch * size.seq), 128), half)),
        ("small_block", pltpu.VMEM((5, small_rows, 128), full)),
        ("small_landing", pltpu.VMEM((members, small_rows, 128), full)),
        ("load_sem", dma((10,))),
        ("x_sem", dma((2,))),
        ("rim_sem", dma((4,))),
        ("own_sem", dma((6,))),
        ("row_sent", dma((depth,))),
        ("row_got", dma((depth,))),
        ("across_sent", dma((depth,))),
        ("across_got", dma((depth,))),
        ("att_sent", dma((size.seq,))),
        ("att_got", dma((size.seq,))),
        ("grad_sent", dma((size.seq,))),
        ("grad_got", dma((size.seq,))),
        ("pair_sent", dma((depth,))),
        ("pair_got", dma((depth,))),
        ("back_sent", dma((depth,))),
        ("back_got", dma((depth,))),
        ("sum_sem", dma((4, len(chunks), slots))),
        ("keep_sem", dma((len(chunks),))),
        ("small_sem", dma((2, slots))),
    ]


def widen_kernel(plan, steps, sums, shift, cotangent, *refs):
    outs = dict(zip(plan, refs[: len(plan)]))
    grad_inputs = refs[len(plan)]
    source, target, moved, kept, result, load_sem, store_sem, row_sem = refs[len(plan) + 1 :]
    rows = shift.shape[0]
    deep = source.shape[0]
    product_rows = source.shape[1]
    width = target.shape[1]

    def load(i):
        return pltpu.make_async_copy(
            sums.at[pl.ds(i * product_rows, product_rows), :], source.at[i % deep],
            load_sem.at[i % deep],
        )

    def store(i):
        name, part = steps[i]
        out = outs[name]
        if out.shape[0] > width:
            out = out.at[pl.ds(part * width, width), :]
        elif out.shape[1] > width:
            out = out.at[:, pl.ds(part * width, width)]
        return pltpu.make_async_copy(target.at[i % deep], out, store_sem.at[i % deep])

    def row_loads(r):
        return (
            pltpu.make_async_copy(shift.at[r], moved.at[r % 2], row_sem.at[0, r % 2]),
            pltpu.make_async_copy(cotangent.at[r], kept.at[r % 2], row_sem.at[1, r % 2]),
        )

    def row_store(r):
        return pltpu.make_async_copy(result.at[r % 2], grad_inputs.at[r], row_sem.at[2, r % 2])

    for i in range(deep - 1):
        load(i).start()
    for copy in row_loads(0):
        copy.start()
    for r in range(rows):
        if r + 1 < rows:
            for copy in row_loads(r + 1):
                copy.start()
        for copy in row_loads(r):
            copy.wait()
        if r >= 2:
            row_store(r - 2).wait()

        def add_rows(b, carry):
            at = pl.ds(pl.multiple_of(b * 64, 64), 64)
            result[r % 2, at, :] = moved[r % 2, at, :].astype(full) + kept[
                r % 2, at, :
            ].astype(full)
            return carry

        lax.fori_loop(0, result.shape[1] // 64, add_rows, 0)
        row_store(r).start()
    for i in range(len(steps)):
        if i + deep - 1 < len(steps):
            load(i + deep - 1).start()
        load(i).wait()
        if i >= deep:
            store(i - deep).wait()

        def convert(b, carry):
            at = pl.multiple_of(b * 64, 64)
            for c in range(product_rows // width):
                target[i % deep, pl.ds(at, 64), c * 128 : (c + 1) * 128] = source[
                    i % deep, pl.ds(c * width + at, 64), :
                ].astype(full)
            return carry

        lax.fori_loop(0, width // 64, convert, 0)
        store(i).start()
    for r in range(max(0, rows - 2), rows):
        row_store(r).wait()
    for i in range(max(0, len(steps) - deep), len(steps)):
        store(i).wait()


def widen(sums, shift, cotangent, shapes, steps):
    any_space = pl.BlockSpec(memory_space=pl.ANY)
    names = tuple(shapes)
    width = shift.shape[2]
    deep = 3
    outs = [jax.ShapeDtypeStruct(shapes[name], full) for name in names]
    outs.append(jax.ShapeDtypeStruct(shift.shape, full))
    row = shift.shape[1:]
    product_rows = sums.shape[0] // len(steps)
    results = pl.pallas_call(
        functools.partial(widen_kernel, names, steps),
        out_shape=outs,
        in_specs=[any_space] * 3,
        out_specs=[any_space] * len(outs),
        scratch_shapes=[
            pltpu.VMEM((deep, product_rows, 128), half),
            pltpu.VMEM((deep, width, width), full),
            pltpu.VMEM((2,) + row, half),
            pltpu.VMEM((2,) + row, half),
            pltpu.VMEM((2,) + row, full),
            pltpu.SemaphoreType.DMA((deep,)),
            pltpu.SemaphoreType.DMA((deep,)),
            pltpu.SemaphoreType.DMA((3, 2)),
        ],
        name="widen",
    )(sums, shift, cotangent)
    return dict(zip(names, results[:-1])), results[-1]


def local(
    inputs,
    cotangent,
    doc_lengths,
    pool_weight,
    pool_bias,
    gain_one,
    shift_one,
    query_weight,
    key_weight,
    value_weight,
    out_weight,
    slopes,
    gain_two,
    shift_two,
    inner_weight,
    inner_bias,
    outer_weight,
    outer_bias,
    up_weight,
    up_bias,
):
    rows, block_len, width = inputs.shape
    hidden = inner_weight.shape[1]
    size = Sizes(
        lax.axis_size("batch"), lax.axis_size("seq"), rows, block_len // 3, width,
        hidden, slopes.shape[0],
    )
    steps = product_list(size.parts)
    product_rows = width * size.lanes
    chunks = [2 * product_rows] * (len(steps) // 2)
    total = len(steps) * product_rows
    vmem = pl.BlockSpec(memory_space=pltpu.VMEM)
    smem = pl.BlockSpec(memory_space=pltpu.SMEM)
    any_space = pl.BlockSpec(memory_space=pl.ANY)
    plan = scratch_plan(size, chunks)
    vectors = (
        pool_bias, gain_one, shift_one, gain_two, shift_two, inner_bias, outer_bias, up_bias,
    )
    output, shift, sums, small = pl.pallas_call(
        functools.partial(layer_kernel, size, chunks, 2),
        out_shape=(
            jax.ShapeDtypeStruct(inputs.shape, half),
            jax.ShapeDtypeStruct(inputs.shape, half),
            jax.ShapeDtypeStruct((total, 128), half),
            jax.ShapeDtypeStruct((small_rows, 128), full),
        ),
        in_specs=[smem, smem] + [vmem] * 8 + [any_space] * 10,
        out_specs=(any_space, any_space, any_space, vmem),
        scratch_shapes=[kind for _, kind in plan],
        compiler_params=pltpu.CompilerParams(
            collective_id=0, has_side_effects=True, vmem_limit_bytes=67043328
        ),
        name="layer",
    )(
        doc_lengths, slopes, *(v.reshape(1, -1) for v in vectors),
        inputs, cotangent, pool_weight, query_weight, key_weight, value_weight,
        out_weight, inner_weight, outer_weight, up_weight,
    )
    shapes = {
        "inner": inner_weight.shape, "outer": outer_weight.shape, "up": up_weight.shape,
        "out": out_weight.shape, "query": query_weight.shape, "key": key_weight.shape,
        "value": value_weight.shape, "pool": pool_weight.shape,
    }
    grads, input_grad = widen(sums, shift, cotangent, shapes, steps)
    places = dict(small_places)

    def vector(name, count):
        at = places[name]
        if count < 128:
            return small[at, :count]
        return small[at : at + count // 128].reshape(count)

    return (
        output,
        input_grad,
        grads["pool"],
        vector("pool_bias", width),
        vector("gain_one", width),
        vector("shift_one", width),
        grads["query"],
        grads["key"],
        grads["value"],
        grads["out"],
        vector("slopes", slopes.shape[0]),
        vector("gain_two", width),
        vector("shift_two", width),
        grads["inner"],
        vector("inner_bias", hidden),
        grads["outer"],
        vector("outer_bias", width),
        grads["up"],
        vector("up_bias", 3 * width),
    )


def solution(mesh):
    blocks = P("batch", "seq", None)
    in_specs = (blocks, blocks, P("batch", None)) + (P(),) * 17
    out_specs = (blocks, blocks) + (P(),) * 17
    return jax.shard_map(local, mesh=mesh, in_specs=in_specs, out_specs=out_specs, check_vma=False)
```

time: 526 us -> 197 us (0.37)
  local copies, waits for them, and re-layouts: 139 us -> 4.76 us
  matrix products: 121 us -> 0 us
  waiting for transfers between devices: 99.3 us -> 0 us
  Pallas kernels: 93.9 us -> 190 us
  other arithmetic: 48.9 us -> 0 us
  between operations: 14.7 us -> 0.7 us
    dot_general x30 -> x0, matrix products: 121 us -> none  [the longest x24 64.1 us: matmul(): return jnp.dot(left, right, preferred_element_type=jnp.float32)]
    pallas_call x1 -> x2, Pallas kernels: 93.9 us -> 190 us  [the longest x1 177 us: local(): pl.pallas_call(functools.partial(layer_kernel, size, chunks, 2), out_shap...]
    unnamed x208 -> x5, local copies, waits for them, and re-layouts: 68.1 us -> 1.15 us
    all_gather x2 -> x0, waiting for transfers between devices: 58.5 us -> none  [the longest x1 29.4 us: local(): lax.all_gather(key_block, 'seq', axis=1, tiled=True)]
    reduce_scatter x2 -> x0, waiting for transfers between devices: 39.9 us -> none  [the longest x1 39.9 us: local(): lax.psum_scatter(grad_value_term.astype(jnp.bfloat16), 'seq', scatter_dim...]
    reduce_sum x10 -> x0, other arithmetic: 23.8 us -> none  [the longest x1 12.7 us: local(): jnp.sum(grad_scores.astype(jnp.float32) * distance[None, None], axis=(0,...]
    reshape x9 -> x4, local copies, waits for them, and re-layouts: 26.6 us -> 3.1 us  [the longest x3 1.8 us: vector(): return small[at:at + count // 128].reshape(count)]
    concatenate x7 -> x0, other arithmetic: 16.4 us -> none  [the longest x6 13.4 us: sum_grads(): out[i] = jnp.concatenate(parts, axis=1)]
  transfers between devices with their start and end apart: 6 -> 0, of which waited for: 4 -> 0; matrix products, arithmetic and copies ran while one was open for 25% -> 0% of each run, Pallas kernels for 0% -> 0%
where the time goes in v2:
time: 197 us; the launch traced here: 196 us
  Pallas kernels  190 us (96%)
  local copies, waits for them, and re-layouts  4.76 us (2%)
    pallas_call x1, Pallas kernels, local(): pl.pallas_call(functools.partial(layer_kernel, size, chunks, 2), out_shap...  177 us
    pallas_call x1, Pallas kernels, widen(): pl.pallas_call(functools.partial(widen_kernel, names, steps), out_shape=o...  13.7 us

profile of v2, /device:TPU:0, one launch (start us, length us, event | category | flops | bytes accessed | tf_op | source)
XLA Modules:
  0.0 195.9 jit_solution(18039838778907577909)
XLA Ops:
  0.7 1.3 reshape.93.up_bias
  2.0 176.7 %layer.1 = (bf16[4,384,512]{2,1,0:T(8,128)(2,1)}, bf16[4,384,512]{2,1,0:T(8,128)(2,1)}, bf16[36864,128]{1,0:T(8,128)(2,1)}, f32[56,128]{1,0:T(8,128)}) custom-call(s32[4,8]{1,0:T(4,128)} %docs.1, f32[8]{0:T(128)} %slopes.1, f32[1,512]{1,0:T(1,128)} %bitcast.26, f32[1,512]{1,0:T(1,128)} %bitcast.27, f32[1,512]{1,0:T(1,128)} %bitcast.28, f32[1,512]{1,0:T(1,128)} %bitcast.29, ...), custom_call_target="tpu_custom_call" | custom-call | tf_op jit(solution)/shard_map/layer/pallas_call | solution.py:1275
  178.7 0.0 copy-start.1
  178.7 0.0 copy-start
  178.7 13.7 %widen.1 = (f32[512,2048]{1,0:T(8,128)}, f32[2048,512]{1,0:T(8,128)}, f32[512,1536]{1,0:T(8,128)}, f32[512,512]{1,0:T(8,128)}, f32[512,512]{1,0:T(8,128)}, /*ind...) custom-call(bf16[36864,128]{1,0:T(8,128)(2,1)} %get-tuple-element.33.sums, ...), custom_call_target="tpu_custom_call" | custom-call | tf_op jit(solution)/shard_map/widen/pallas_call | solution.py:1216
  192.4 0.0 copy-done.1
  192.5 0.6 slice_bitcast_fusion.2
  193.1 0.6 slice_bitcast_fusion
  193.7 0.6 slice_bitcast_fusion.1
  194.3 0.5 slice_bitcast_fusion.8
  194.8 0.0 copy-done
  194.8 1.1 copy.40
Async XLA Ops:
  178.7 13.8 %copy-start.1 = (f32[56,128]{1,0:T(8,128)S(1)}, f32[56,128]{1,0:T(8,128)}, u32[]{:S(2)}) copy-start(f32[56,128]{1,0:T(8,128)} %get-tuple-element.37) | copy-start | bytes 86020
  178.7 16.1 %copy-start = (bf16[4,384,512]{2,1,0:T(8,128)(2,1)S(1)}, bf16[4,384,512]{2,1,0:T(8,128)(2,1)}, u32[]{:S(2)}) copy-start(bf16[4,384,512]{2,1,0:T(8,128)(2,1)} %get-tuple-element.70) | copy-start | bytes 4718596

commit v3 on v2

v3 whole, which is shorter than its diff:
```python
import functools
import math
from types import SimpleNamespace

import jax
import jax.numpy as jnp
from jax import lax
from jax.experimental import pallas as pl
from jax.experimental.pallas import tpu as pltpu
from jax.sharding import PartitionSpec as P

norm_eps = 1e-05
log2_e = math.log2(math.e)

MESH = pl.DeviceIdType.MESH
half = jnp.bfloat16
full = jnp.float32


class Place:
    def __init__(self, batch_size, seq_size):
        side = math.isqrt(batch_size)
        self.depth = seq_size // 2
        self.batch = lax.axis_index("batch")
        self.seq = lax.axis_index("seq")
        self.core = self.seq % 2
        self.level = self.seq // 2
        high, low = self.batch // side, self.batch % side
        self.first = jnp.where(self.core == 0, low, high)
        self.second = jnp.where(self.core == 0, high, low)
        self.side = side
        self.sizes = stage_sizes(batch_size, seq_size)
        bits = [self.level // 2**b % 2 for b in range(len(self.sizes) - 3)]
        self.where = (self.core, self.first, self.second, *bits)

    def batch_at(self, first, second):
        return jnp.where(
            self.core == 0, second * self.side + first, first * self.side + second
        )

    def partner(self, stage, step):
        member = (self.where[stage] + step) % self.sizes[stage]
        if stage == 0:
            return (self.batch, self.level * 2 + member)
        if stage == 1:
            return (self.batch_at(member, self.second), self.seq)
        if stage == 2:
            return (self.batch_at(self.first, member), self.seq)
        other = self.level + (member - self.where[stage]) * 2 ** (stage - 3)
        return (self.batch, other * 2 + self.core)


def stage_sizes(batch_size, seq_size):
    side = math.isqrt(batch_size)
    bits = (seq_size // 2).bit_length() - 1
    return (2, side, side) + (2,) * bits


def sum_slots(batch_size, seq_size):
    return sum(size - 1 for size in stage_sizes(batch_size, seq_size))


class SumPieces:
    def __init__(self, place, chunks, orders, mine, landing, piece, out, sems, keep):
        self.place, self.chunks, self.orders = place, chunks, orders
        self.mine, self.landing, self.piece, self.out = mine, landing, piece, out
        self.keep = keep
        self.sent, self.got, self.back_sent, self.back_got = sems
        self.starts = [sum(chunks[:c]) for c in range(len(chunks))]
        sizes = place.sizes
        self.last = len(sizes) - 1
        self.events = 2 * len(sizes) + 1
        self.land = {}
        at = 0
        for c in range(len(chunks)):
            for stage in range(len(sizes)):
                for step in self.steps(c, stage):
                    self.land[c, stage, step] = at
                    at += self.rows(c, stage)

    @staticmethod
    def landing_rows(batch_size, seq_size, chunks, orders):
        sizes, rows = stage_sizes(batch_size, seq_size), 0
        for left, order in zip(chunks, orders):
            for axis in order:
                left //= sizes[axis]
                rows += left * (sizes[axis] - 1)
        return rows

    def size_at(self, c, stage):
        return self.place.sizes[self.orders[c][stage]]

    def where_at(self, c, stage):
        return self.place.where[self.orders[c][stage]]

    def slot(self, c, stage):
        return sum(self.size_at(c, t) - 1 for t in range(stage))

    def rows(self, c, stage):
        count = self.chunks[c]
        for t in range(stage + 1):
            count //= self.size_at(c, t)
        return count

    def begin(self, c, stage):
        at = self.starts[c]
        for t in range(stage):
            at = at + self.where_at(c, t) * self.rows(c, t)
        return at

    def scatter(self, c, stage, step):
        count = self.rows(c, stage)
        member = (self.where_at(c, stage) + step) % self.size_at(c, stage)
        at = pl.multiple_of(self.begin(c, stage) + member * count, 16)
        slot = self.slot(c, stage) + step - 1
        return pltpu.make_async_remote_copy(
            src_ref=self.mine.at[pl.ds(at, count), :],
            dst_ref=self.landing.at[pl.ds(self.land[c, stage, step], count), :],
            send_sem=self.sent.at[c, slot],
            recv_sem=self.got.at[c, slot],
            device_id=self.place.partner(self.orders[c][stage], step),
            device_id_type=MESH,
        )

    def piece_span(self, c):
        count = self.rows(c, self.last)
        return pl.ds(self.starts[c] * count // self.chunks[c], count)

    def keep_copy(self, c):
        at = pl.multiple_of(self.begin(c, self.last + 1), 16)
        return pltpu.make_async_copy(
            self.piece.at[self.piece_span(c), :],
            self.out.at[pl.ds(at, self.rows(c, self.last)), :],
            self.keep.at[c],
        )

    def gather(self, c, stage, step):
        count = self.rows(c, stage)
        at = pl.multiple_of(self.begin(c, stage + 1), 16)
        slot = self.slot(c, stage) + step - 1
        source = self.out.at[pl.ds(at, count), :]
        if stage == self.last:
            source = self.piece.at[self.piece_span(c), :]
        return pltpu.make_async_remote_copy(
            src_ref=source,
            dst_ref=self.out.at[pl.ds(at, count), :],
            send_sem=self.back_sent.at[c, slot],
            recv_sem=self.back_got.at[c, slot],
            device_id=self.place.partner(self.orders[c][stage], step),
            device_id_type=MESH,
        )

    def add(self, c, stage):
        count = self.rows(c, stage)
        at = self.begin(c, stage + 1)
        part = min(count, 512)

        def body(i, carry):
            here = pl.ds(pl.multiple_of(at + i * part, 16), part)
            if self.size_at(c, stage) == 2:
                there = pl.multiple_of(self.land[c, stage, 1] + i * part, 16)
                total = self.mine[here, :] + self.landing[pl.ds(there, part), :]
            else:
                total = self.mine[here, :].astype(full)
                for step in self.steps(c, stage):
                    there = pl.multiple_of(self.land[c, stage, step] + i * part, 16)
                    total = total + self.landing[pl.ds(there, part), :].astype(full)
                total = total.astype(half)
            if stage == self.last:
                first = self.piece_span(c).start
                self.piece[pl.ds(pl.multiple_of(first + i * part, 16), part), :] = total
            else:
                self.mine[here, :] = total
            return carry

        lax.fori_loop(0, count // part, body, 0)

    def steps(self, c, stage):
        return range(1, self.size_at(c, stage))

    def advance(self, c, event):
        count = self.last + 1
        if 1 <= event <= count:
            for step in self.steps(c, event - 1):
                self.scatter(c, event - 1, step).wait_recv()
            self.add(c, event - 1)
        if event < count:
            for step in self.steps(c, event):
                self.scatter(c, event, step).start()
            return
        stage = 2 * count - 1 - event
        if event == count:
            self.keep_copy(c).start()
        else:
            for step in self.steps(c, stage + 1):
                self.gather(c, stage + 1, step).wait_recv()
        if event == count + 1:
            self.keep_copy(c).wait()
        if stage >= 0:
            for step in self.steps(c, stage):
                self.gather(c, stage, step).start()

    def finish(self):
        for c in range(len(self.chunks)):
            for stage in range(self.last + 1):
                for step in self.steps(c, stage):
                    self.scatter(c, stage, step).wait_send()
                    self.gather(c, stage, step).wait_send()


class SumSmall:
    def __init__(self, place, block, landing, sems):
        self.place, self.block, self.landing = place, block, landing
        self.sent, self.got = sems
        sizes = place.sizes
        self.slot = [sum(s - 1 for s in sizes[:stage]) for stage in range(len(sizes))]
        self.base = [sum(sizes[:stage]) for stage in range(len(sizes))]

    def copy(self, stage, step):
        slot = self.slot[stage] + step - 1
        return pltpu.make_async_remote_copy(
            src_ref=self.block.at[stage],
            dst_ref=self.landing.at[self.base[stage] + self.place.where[stage]],
            send_sem=self.sent.at[slot],
            recv_sem=self.got.at[slot],
            device_id=self.place.partner(stage, step),
            device_id_type=MESH,
        )

    def send(self, stage):
        self.landing[self.base[stage] + self.place.where[stage]] = self.block[stage]
        for step in range(1, self.place.sizes[stage]):
            self.copy(stage, step).start()

    def receive(self, stage):
        for step in range(1, self.place.sizes[stage]):
            self.copy(stage, step).wait_recv()
        total = self.landing[self.base[stage]]
        for member in range(1, self.place.sizes[stage]):
            total = total + self.landing[self.base[stage] + member]
        self.block[stage + 1] = total

    def finish(self):
        for stage in range(len(self.place.sizes)):
            for step in range(1, self.place.sizes[stage]):
                self.copy(stage, step).wait_send()


def dot_nn(left, right):
    return lax.dot_general(
        left, right, (((1,), (0,)), ((), ())), preferred_element_type=full
    )


def dot_nt(left, right):
    return lax.dot_general(
        left, right, (((1,), (1,)), ((), ())), preferred_element_type=full
    )


def dot_tn(left, right):
    return lax.dot_general(
        left, right, (((0,), (0,)), ((), ())), preferred_element_type=full
    )


def centred_rows(values_in):
    centre = values_in - jnp.mean(values_in, axis=-1, keepdims=True)
    spread = jnp.mean(centre * centre, axis=-1, keepdims=True)
    inverse = lax.rsqrt(spread + norm_eps)
    return centre * inverse, inverse


def norm_back(grad_normed, scaled, inverse, gain):
    inner = grad_normed * gain
    first = jnp.mean(inner, axis=-1, keepdims=True)
    second = jnp.mean(inner * scaled, axis=-1, keepdims=True)
    return inverse * (inner - first - scaled * second)


class Sizes:
    def __init__(self, batch_size, seq_size, rows, block, width, hidden, heads):
        self.batch, self.seq = batch_size, seq_size
        self.rows, self.block, self.width, self.hidden = rows, block, width, hidden
        self.heads = heads
        self.tokens = rows * block
        self.length = seq_size * block
        self.depth = seq_size // 2
        self.per_row = seq_size // rows
        self.chips_per_row = self.per_row // 2
        self.own_width = width // self.per_row
        self.own_heads = heads // self.per_row
        self.pairs = self.own_heads // 2
        self.head_dim = width // heads
        self.span = 2 * block
        self.query_blocks = self.length // self.span
        self.reach = self.query_blocks // 2
        self.tiles = []
        for i in range(self.query_blocks):
            for j in range(max(0, i - self.reach), i + 1):
                self.tiles.append((i, j))
        self.lanes = width // 128
        self.parts = hidden // width


def product_list(parts):
    order = []
    for j in range(parts):
        order += [(Product.inner, j), (Product.outer, j)]
    order += [(Product.up, 0), (Product.up, 1), (Product.up, 2), (Product.out, 0)]
    order += [(Product.query, 0), (Product.key, 0), (Product.value, 0)]
    order += [(Product.pool, 0), (Product.pool, 1), (Product.pool, 2)]
    return order


class Product:
    inner, outer, up, out, query, key, value, pool = range(8)


class Small:
    pool_bias, gain_one, shift_one, slopes = 0, 4, 8, 12
    gain_two, shift_two, inner_bias, outer_bias, up_bias = 13, 17, 21, 37, 41


class Site:
    feed, norm_two, second, up, out, rise, heads, back, settle = range(9)
    pair, give, weights, rows, norm_one, pool = range(9, 15)


small_rows = 56


pace = {
    (Site.feed, 0): (0,),
    (Site.feed, 1): (1,),
    (Site.feed, 2): (0, 2,),
    (Site.feed, 3): (1, 3,),
    (Site.norm_two, 0): (2,),
    (Site.norm_two, 1): (0,),
    (Site.norm_two, 2): (3,),
    (Site.second, 0): (1,),
    (Site.up, 1): (4,),
    (Site.up, 2): (2,),
    (Site.out, 0): (5,),
    (Site.rise, 0): (0,),
    (Site.rise, 3): (4,),
    (Site.heads, 0): (3, 5, 1, 2, 0,),
    (Site.back, 3): (1,),
    (Site.back, 4): (4, 2, 3, 0,),
    (Site.back, 6): (1, 5,),
    (Site.back, 7): (2, 4, 3,),
    (Site.settle, 0): (0,),
    (Site.pair, 0): (1, 5,),
    (Site.pair, 3): (2,),
    (Site.give, 0): (4,),
    (Site.give, 2): (3, 0,),
    (Site.weights, 0): (1,),
    (Site.weights, 1): (6,),
    (Site.weights, 2): (5,),
    (Site.rows, 0): (2, 0, 1, 6, 2, 0,),
    (Site.norm_one, 1): (0,),
    (Site.norm_one, 2): (1,),
    (Site.pool, 0): (7,),
    (Site.pool, 1): (6, 8,),
    (Site.pool, 2): (4, 1, 3, 9,),
}
finish_order = (
    5, 7, 2, 8, 6, 9, 4, 2, 3, 5, 7, 6, 8, 4, 9, 5,
    3, 6, 7, 8, 6, 4, 7, 9, 8, 5, 6, 9, 7, 3, 8, 9,
    3, 7, 8, 4, 9, 4, 7, 8, 5, 9, 6, 5, 7, 8, 9, 6,
    6, 7, 8, 7, 8, 9, 9,
)
level_first = ()


def axis_orders(size, count):
    axes = tuple(range(len(stage_sizes(size.batch, size.seq))))
    return [
        axes[:2] + axes[3:] + axes[2:3] if c in level_first else axes for c in range(count)
    ]


def layer_kernel(size, chunks, docs, slopes, pool_bias, gain_one, shift_one,
                 gain_two, shift_two, inner_bias, outer_bias, up_bias,
                 inputs_hbm, cotangent_hbm, pool_hbm, query_hbm, key_hbm, value_hbm,
                 out_hbm, inner_hbm, outer_hbm, up_hbm,
                 output_hbm, shift_hbm, sums_hbm, small_out,
                 *scratch_refs):
    s = SimpleNamespace(**dict(zip(scratch_plan(size, chunks), scratch_refs)))
    place = Place(size.batch, size.seq)
    me, core, level = place.seq, place.core, place.level
    rows, block, width, hidden = size.rows, size.block, size.width, size.hidden
    tokens, length, depth = size.tokens, size.length, size.depth
    per_row, chips = size.per_row, size.chips_per_row
    own_width, pairs = size.own_width, size.pairs
    my_row, my_group = me // per_row, me % per_row
    lanes, parts, span = size.lanes, size.parts, size.span
    products = product_list(parts)
    product_rows = width * lanes

    def tile_at(name, part, lane):
        return products.index((name, part)) * product_rows + lane * width

    loads = SimpleNamespace()

    def load(source, target):
        copy = pltpu.make_async_copy(source, target, s.load_sem.at[len(vars(loads))])
        copy.start()
        return copy

    first_column = pl.multiple_of(my_group * own_width, own_width)

    def x_load(step):
        return pltpu.make_async_copy(
            inputs_hbm.at[(my_row + 1 + step) % rows], s.x.at[step % 2],
            s.x_sem.at[step % 2],
        )

    x_load(0).start()
    loads.pool = load(pool_hbm, s.pool_w)
    loads.dy = load(cotangent_hbm, s.raised)
    loads.up = load(up_hbm, s.up_w)
    loads.query = load(query_hbm.at[:, pl.ds(first_column, own_width)], s.query_w)
    loads.key = load(key_hbm.at[:, pl.ds(first_column, own_width)], s.key_w)
    loads.value = load(value_hbm.at[:, pl.ds(first_column, own_width)], s.value_w)
    loads.outer = load(outer_hbm, s.outer_w)
    loads.out = load(out_hbm, s.out_w)
    loads.inner = load(inner_hbm, s.inner_w)

    barrier = pltpu.get_barrier_semaphore()
    greeted = [(place.batch, (me + k) % size.seq) for k in range(1, size.seq)]
    for stage in (1, 2):
        greeted += [place.partner(stage, k) for k in range(1, place.sizes[stage])]
    for device in greeted:
        pl.semaphore_signal(barrier, inc=1, device_id=device, device_id_type=MESH)
    pl.semaphore_wait(barrier, len(greeted))

    def remote(source, target, sent, got, device):
        return pltpu.make_async_remote_copy(
            src_ref=source, dst_ref=target, send_sem=sent, recv_sem=got,
            device_id=device, device_id_type=MESH,
        )

    rim_copy = remote(
        inputs_hbm.at[:, pl.ds(3 * block - 16, 16), :], s.rim,
        s.rim_sem.at[0], s.rim_sem.at[1], (place.batch, (me + 1) % size.seq),
    )

    @pl.when(me < size.seq - 1)
    def _():
        rim_copy.start()

    small_block = s.small_block
    small_block[0] = jnp.zeros((small_rows, 128), full)

    def put_small(name, at, values):
        for c in range(values.shape[1] // 128):
            small_block[0, pl.ds(name + at // 128 + c, 1), :] = values[
                :, c * 128 : (c + 1) * 128
            ]

    stage = s.stage

    def spread_rows(at, values):
        for c in range(lanes):
            stage[c, pl.ds(at, values.shape[0]), :] = values[:, c * 128 : (c + 1) * 128]

    def every_third(at):
        return jnp.concatenate(
            [stage[c, pl.ds(at, block, stride=3), :] for c in range(lanes)], axis=1
        )

    def put_third(at, values):
        for c in range(lanes):
            stage[c, pl.ds(at, block, stride=3), :] = values[:, c * 128 : (c + 1) * 128]

    def row_span(r):
        return pl.ds(pl.multiple_of(r * block, block), block)

    loads.dy.wait()
    loads.up.wait()
    up_sum = jnp.zeros((1, width), full)

    def split_cotangent(r, carry):
        spread_rows(8, s.raised[r].astype(full))
        totals = []
        grad = jnp.zeros((block, width), full)
        for k in range(3):
            part = every_third(8 + k)
            totals.append(carry[k] + jnp.sum(part, axis=0, keepdims=True))
            low = part.astype(half)
            s.dy[row_span(r), k * width : (k + 1) * width] = low
            grad = grad + dot_nt(low, s.up_w[:, k * width : (k + 1) * width])
        s.grad_resid[row_span(r), :] = grad
        low = grad.astype(half)
        s.grad_branch[row_span(r), :] = low
        totals.append(carry[3] + jnp.sum(low.astype(full), axis=0, keepdims=True))
        return tuple(totals)

    sums = lax.fori_loop(0, rows, split_cotangent, (up_sum,) * 4)
    loads.x = load(inputs_hbm, s.raised)
    for k in range(3):
        put_small(Small.up_bias, k * width, sums[k])
    put_small(Small.outer_bias, 0, sums[3])

    @pl.when(me > 0)
    def _():
        rim_copy.wait_recv()

    loads.pool.wait()
    nr = s.nr

    def nr_rows(owner):
        return pl.ds(pl.multiple_of(owner * block, block), block)

    def row_copy(r, target_level):
        return remote(
            s.normed.at[row_span(r), :], nr.at[nr_rows(me), :],
            s.row_sent.at[target_level], s.row_got.at[level],
            (place.batch, target_level * 2 + core),
        )

    def row_from(source_level):
        return remote(
            s.normed.at[row_span(0), :], nr.at[nr_rows(source_level * 2 + core), :],
            s.row_sent.at[source_level], s.row_got.at[source_level],
            (place.batch, source_level * 2 + core),
        )

    for step in range(rows):
        r = (my_row + 1 + step) % rows
        rim_rows = s.rim[r].astype(full)[8:16, :]
        rim_rows = jnp.where(me > 0, rim_rows, 0.0)
        spread_rows(0, rim_rows)
        x_load(step).wait()
        if step + 1 < rows:
            x_load(step + 1).start()
        spread_rows(8, s.x[step % 2].astype(full))
        pooled = jnp.zeros((block, width), full) + pool_bias[...]
        for k in range(3):
            part = every_third(6 + k).astype(half)
            s.groups[row_span(r), k * width : (k + 1) * width] = part
            pooled = pooled + dot_nn(part, s.pool_w[k * width : (k + 1) * width, :])
        s.pooled[row_span(r), :] = pooled
        scaled, _ = centred_rows(pooled)
        s.normed[row_span(r), :] = (scaled * gain_one[...] + shift_one[...]).astype(half)
        if step < rows - 1:
            for i in range(chips):
                row_copy(r, r * chips + i).start()
        else:
            for i in range(1, chips):
                row_copy(r, r * chips + (level % chips + i) % chips).start()
            own_copy = pltpu.make_async_copy(
                s.normed.at[row_span(r), :], nr.at[nr_rows(me), :], s.own_sem.at[0]
            )
            own_copy.start()

    loads.outer.wait()

    def before_activation(j, carry):
        at = pl.ds(pl.multiple_of(j * width, width), width)
        grad = dot_nt(s.grad_branch[...], s.outer_w[at, :])
        s.grad_inner[:, at] = grad.astype(half)
        return carry

    lax.fori_loop(0, parts, before_activation, 0)

    def across(source_level, owner_core):
        owner = source_level * 2 + owner_core
        return remote(
            nr.at[nr_rows(owner), :], nr.at[nr_rows(owner), :],
            s.across_sent.at[source_level], s.across_got.at[source_level],
            (place.batch, level * 2 + 1 - core),
        )

    loads.query.wait()
    loads.key.wait()
    loads.value.wait()

    def project(owner):
        at = nr_rows(owner)
        source = nr[at, :]
        q = dot_nn(source, s.query_w[...])
        k = dot_nn(source, s.key_w[...])
        v = dot_nn(source, s.value_w[...])
        qt, kt, vt = q.T, k.T, v.T
        s.vt[:, at] = vt.astype(half)
        zeros = jnp.zeros((64, block), half)
        line = lax.broadcasted_iota(jnp.int32, (16, block), 0)
        key_at = owner * block + lax.broadcasted_iota(jnp.int32, (16, block), 1)
        fine = (key_at % 128).astype(full)
        coarse = (key_at - key_at % 128).astype(full)
        extra = jnp.where(line == 0, 1.0, jnp.where(line == 1, fine, coarse))
        extra = jnp.where(line < 3, extra, 0.0).astype(half)
        for p in range(pairs):
            s.k[p, at, :] = k[:, p * 128 : (p + 1) * 128].astype(half)
            s.v[p, at, :] = v[:, p * 128 : (p + 1) * 128].astype(half)
            for side in range(2):
                h = 2 * p + side
                piece = qt[h * 64 : (h + 1) * 64, :].astype(half)
                s.qt[h, :, at] = jnp.concatenate(
                    [piece, zeros] if side == 0 else [zeros, piece], axis=0
                )
                piece = kt[h * 64 : (h + 1) * 64, :].astype(half)
                s.kt[h, :, at] = jnp.concatenate([piece, extra], axis=0)

    order = [0]
    for k in range(1, depth):
        order.append((k + 1) // 2 if k % 2 else depth - k // 2)
    for k in order:
        source_level = (level + k) % depth
        if k == 0:
            own_copy.wait()
        else:
            row_from(source_level).wait_recv()
        across(source_level, core).start()
    for k in order:
        source_level = (level + k) % depth
        project(source_level * 2 + core)
        across(source_level, 1 - core).wait_recv()
        project(source_level * 2 + 1 - core)

    ends = []
    total = 0
    for d in range(docs.shape[1]):
        total = total + docs[my_row, d]
        ends.append(total)
    key_line = lax.broadcasted_iota(jnp.int32, (span, span), 0)
    query_line = lax.broadcasted_iota(jnp.int32, (span, span), 1)
    scale_two = size.head_dim ** -0.5 * log2_e

    def tile_of(i, j):
        return size.tiles.index((i, j))

    def near(i):
        return range(max(0, i - size.reach), i + 1)

    def att_copy(owner, at_row, at_group, slot):
        return remote(
            s.att_out.at[nr_rows(owner), :],
            s.att.at[row_span(at_row), pl.ds(pl.multiple_of(at_group * own_width, own_width), own_width)],
            s.att_sent.at[owner], s.att_got.at[slot], (place.batch, owner),
        )

    def head_slope(h):
        return slopes[my_group * size.own_heads + h]

    for i in range(size.query_blocks):
        cols = slice(i * span, (i + 1) * span)
        place_q = 3 * (i * span + lax.broadcasted_iota(jnp.int32, (1, span), 1))
        start = jnp.zeros((1, span), jnp.int32)
        for end in ends:
            start = jnp.where(end <= place_q, jnp.maximum(start, end), start)
        for w, j in enumerate(near(i)):
            allowed = 3 * (j * span + key_line) >= start
            if j == i:
                allowed = allowed & (key_line <= query_line)
            s.work[size.reach + 1 + w] = jnp.where(allowed, 0.0, -1e30)

        def forward_pair(p, carry):
            for side in range(2):
                h = 2 * p + side
                slope_two = head_slope(h) * log2_e
                top = None
                for w, j in enumerate(near(i)):
                    score = dot_nn(s.k[p, j * span : (j + 1) * span, :], s.qt[h, :, cols])
                    away = (key_line + (j - i) * span).astype(full)
                    score = score * scale_two + (away * slope_two + s.work[size.reach + 1 + w])
                    s.work[w] = score
                    best = jnp.max(score, axis=0, keepdims=True)
                    top = best if top is None else jnp.maximum(top, best)
                total = jnp.zeros((1, span), full)
                mixed = jnp.zeros((64, span), full)
                for w, j in enumerate(near(i)):
                    expo = jnp.exp2(s.work[w] - top)
                    total = total + jnp.sum(expo, axis=0, keepdims=True)
                    low = expo.astype(half)
                    s.expo[h, tile_of(i, j)] = low
                    at = pl.multiple_of(h * 64, 64)
                    mixed = mixed + dot_nn(
                        s.vt[pl.ds(at, 64), j * span : (j + 1) * span], low
                    )
                inverse = 1.0 / total
                s.inverse[h, :, cols] = jnp.broadcast_to(inverse, (8, span))
                s.mixed[pl.ds(pl.multiple_of(h * 64, 64), 64), cols] = mixed * inverse
            return carry

        lax.fori_loop(0, pairs, forward_pair, 0)
        s.att_out[cols, :] = s.mixed[:, cols].T.astype(half)
        for owner in (2 * i, 2 * i + 1):

            @pl.when(me == owner)
            def _():
                copy = pltpu.make_async_copy(
                    s.att_out.at[nr_rows(owner), :],
                    s.att.at[row_span(my_row), pl.ds(first_column, own_width)],
                    s.own_sem.at[1],
                )
                copy.start()

            @pl.when(me != owner)
            def _():
                att_copy(owner, my_row, my_group, me).start()

    loads.out.wait()
    loads.inner.wait()
    pltpu.make_async_copy(
        s.att_out.at[nr_rows(0), :],
        s.att.at[row_span(my_row), pl.ds(first_column, own_width)],
        s.own_sem.at[1],
    ).wait()
    for k in range(1, size.seq):
        source = (me + k) % size.seq
        att_copy(source, source // per_row, source % per_row, source).wait_recv()

    def second_norm(r, carry):
        at = row_span(r)
        residual = s.pooled[at, :] + dot_nn(s.att[at, :], s.out_w[...])
        s.residual[at, :] = residual
        scaled, _ = centred_rows(residual)
        s.normed_two[at, :] = (scaled * gain_two[...] + shift_two[...]).astype(half)
        return carry

    lax.fori_loop(0, rows, second_norm, 0)

    big = SumPieces(place, chunks, axis_orders(size, len(chunks)), s.mine, s.landing, s.piece, sums_hbm,
                    [s.sum_sem.at[k] for k in range(4)], s.keep_sem)
    reached = [0] * len(chunks)
    visits = {}
    split = len(chunks) * 2 * product_rows > sum(chunks)
    chunk_of = {name: name for name in range(len(chunks))}
    if not split:
        del chunk_of[len(chunks) - 1]
        chunk_of[len(chunks)] = len(chunks) - 1

    def sum_step(c):
        big.advance(c, reached[c])
        reached[c] += 1

    def ticks(where):
        visit = visits.get(where, 0)
        visits[where] = visit + 1
        for name in pace.get((where, visit), ()):
            if name in chunk_of:
                sum_step(chunk_of[name])

    def put_product(at, value):
        for c in range(value.shape[1] // 128):
            s.mine[pl.ds(at + c * width, width), :] = value[
                :, c * 128 : (c + 1) * 128
            ].astype(half)

    for j in range(parts):
        at = slice(j * width, (j + 1) * width)

        def feed(r, carry):
            here = row_span(r)
            value = dot_nn(s.normed_two[here, :], s.inner_w[:, at]) + inner_bias[:, at]
            share = 0.5 + 0.5 * lax.erf(value * (0.5 ** 0.5))
            density = jnp.exp(-0.5 * value * value) * (0.5 / math.pi) ** 0.5
            s.activated[here, at] = (value * share).astype(half)
            grad = s.grad_inner[here, at].astype(full) * (share + value * density)
            low = grad.astype(half)
            s.grad_inner[here, at] = low
            return carry + jnp.sum(low.astype(full), axis=0, keepdims=True)

        total = lax.fori_loop(0, rows, feed, jnp.zeros((1, width), full))
        put_small(Small.inner_bias, j * width, total)
        put_product(tile_at(Product.inner, j, 0), dot_tn(s.normed_two[...], s.grad_inner[:, at]))
        put_product(tile_at(Product.outer, j, 0), dot_tn(s.activated[:, at], s.grad_branch[...]))
        ticks(Site.feed)

    def grad_copy(owner, slot):
        row, group = owner // per_row, owner % per_row
        column = pl.ds(pl.multiple_of(group * own_width, own_width), own_width)
        return remote(
            s.grad_att.at[row_span(row), column], s.grad_heads.at[nr_rows(slot), :],
            s.grad_sent.at[owner], s.grad_got.at[slot], (place.batch, owner),
        )

    gain_sum = jnp.zeros((1, width), full)
    shift_sum = jnp.zeros((1, width), full)
    for step in range(rows):
        r = (my_row + 1 + step) % rows
        at = row_span(r)
        grad = dot_nt(s.grad_inner[at, :], s.inner_w[...])
        scaled, inverse = centred_rows(s.residual[at, :])
        gain_sum = gain_sum + jnp.sum(grad * scaled, axis=0, keepdims=True)
        shift_sum = shift_sum + jnp.sum(grad, axis=0, keepdims=True)
        mixed = s.grad_resid[at, :] + norm_back(grad, scaled, inverse, gain_two[...])
        s.grad_resid[at, :] = mixed
        s.grad_att[at, :] = dot_nt(mixed.astype(half), s.out_w[...]).astype(half)
        for g in range(per_row):
            owner = r * per_row + g
            if step < rows - 1:
                grad_copy(owner, me).start()
            else:

                @pl.when(owner != me)
                def _():
                    grad_copy(owner, me).start()

                @pl.when(owner == me)
                def _():
                    pltpu.make_async_copy(
                        s.grad_att.at[row_span(my_row), pl.ds(first_column, own_width)],
                        s.grad_heads.at[nr_rows(me), :], s.own_sem.at[2],
                    ).start()
        ticks(Site.norm_two)
    put_small(Small.gain_two, 0, gain_sum)
    put_small(Small.shift_two, 0, shift_sum)

    def second_residual(r, carry):
        at = row_span(r)
        value = s.residual[at, :] + dot_nn(s.activated[at, :], s.outer_w[...])
        s.normed_two[at, :] = (value + outer_bias[...]).astype(half)
        return carry

    for r in range(rows):
        second_residual(r, 0)
        ticks(Site.second)
    for k in range(3):
        at = slice(k * width, (k + 1) * width)
        put_product(tile_at(Product.up, k, 0), dot_tn(s.normed_two[...], s.dy[:, at]))
        ticks(Site.up)
    put_product(tile_at(Product.out, 0, 0), dot_tn(s.att[...], s.grad_resid[...].astype(half)))
    ticks(Site.out)

    up_row = jnp.concatenate(
        [up_bias[c : c + 128].reshape(1, 128) for c in range(0, 3 * width, 128)], axis=1
    )

    def raise_row(r, carry):
        for k in range(3):
            at = slice(k * width, (k + 1) * width)
            raised = dot_nn(s.normed_two[row_span(r), :], s.up_w[:, at])
            put_third(8 + k, raised + up_row[:, at])
        whole = jnp.concatenate([stage[c, 8 : 8 + 3 * block, :] for c in range(lanes)], axis=1)
        s.raised[r] = (s.raised[r].astype(full) + whole).astype(half)
        return carry

    loads.x.wait()
    for r in range(rows):
        raise_row(r, 0)
        ticks(Site.rise)
    output_copy = pltpu.make_async_copy(s.raised, output_hbm, s.own_sem.at[3])
    output_copy.start()

    blank = jnp.zeros((width, 128), half)
    for name in (Product.query, Product.key, Product.value):
        for c in range(lanes):
            s.mine[pl.ds(tile_at(name, 0, c), width), :] = blank

    pltpu.make_async_copy(
        s.grad_att.at[row_span(my_row), pl.ds(first_column, own_width)],
        s.grad_heads.at[nr_rows(me), :], s.own_sem.at[2],
    ).wait()
    ticks(Site.heads)
    for k in range(1, size.seq):
        grad_copy((me + k) % size.seq, (me + k) % size.seq).wait_recv()

    half_blocks = size.query_blocks // 2

    def value_tile(p, j):
        lane = pl.multiple_of((p * half_blocks + j // 2) * 128, 128)
        return s.residual.at[(j % 2) * span : (j % 2 + 1) * span, pl.ds(lane, 128)]

    def value_block(p, b):
        lane = pl.multiple_of((p * half_blocks + b // 4) * 128, 128)
        return s.residual.at[row_span(b % 4), pl.ds(lane, 128)]

    def key_tile(p, j):
        at = p * half_blocks + j // 2
        return s.work.at[at, :, (j % 2) * 128 : (j % 2 + 1) * 128]

    def key_block(p, b):
        lane = pl.multiple_of(b // 2 % 2 * 128, 128)
        return s.work.at[p * half_blocks + b // 4, row_span(b % 2), pl.ds(lane, 128)]

    turned = s.work.at[2 * size.reach + 1, 0:own_width, :]

    for i in range(size.query_blocks):
        cols = slice(i * span, (i + 1) * span)
        turned[...] = s.grad_heads[cols, :].astype(full).T
        query_at = (i * span + lax.broadcasted_iota(jnp.int32, (1, span), 1)).astype(full)

        def backward_pair(p, carry):
            for side in range(2):
                h = 2 * p + side
                head = pl.ds(pl.multiple_of(h * 64, 64), 64)
                inverse = s.inverse[h, 0:1, cols]
                grad = turned[head, :] * inverse
                term = jnp.sum(grad * s.mixed[head, cols], axis=0, keepdims=True)
                low = grad.astype(half)
                zeros = jnp.zeros((64, span), half)
                low = jnp.concatenate([low, zeros] if side == 0 else [zeros, low], axis=0)
                query_grad = jnp.zeros((80, span), full)
                for j in near(i):
                    keys = slice(j * span, (j + 1) * span)
                    expo = s.expo[h, tile_of(i, j)]
                    grad_probs = dot_nn(s.v[p, keys, :], low)
                    grad_scores = (expo.astype(full) * (grad_probs - term)).astype(half)
                    to_value = dot_nt(expo, low)
                    to_key = dot_nt(grad_scores, s.qt[h, :, cols])
                    if j == i and side == 0:
                        value_tile(p, j)[...] = to_value
                        key_tile(p, j)[...] = to_key
                    else:
                        value_tile(p, j)[...] += to_value
                        key_tile(p, j)[...] += to_key
                    query_grad = query_grad + dot_nn(s.kt[h, :, keys], grad_scores)
                s.mixed[head, cols] = query_grad[:64, :]
                slope = (
                    query_grad[65:66, :] + query_grad[66:67, :] - query_at * query_grad[64:65, :]
                )
                slope = jnp.broadcast_to(slope, (8, span))
                if i == 0:
                    s.slope_sum[h] = slope
                else:
                    s.slope_sum[h] += slope
            return carry

        for p in range(pairs):
            backward_pair(p, 0)
            ticks(Site.back)

    head_lane = lax.broadcasted_iota(jnp.int32, (1, 128), 1)
    slope_row = jnp.zeros((1, 128), full)
    for h in range(size.own_heads):
        total = jnp.sum(s.slope_sum[h][0:1, :], axis=1, keepdims=True)
        slope_row = slope_row + jnp.where(head_lane == my_group * size.own_heads + h, total, 0.0)
    small_block[0, pl.ds(Small.slopes, 1), :] = slope_row

    scale = size.head_dim ** -0.5

    fit = width // own_width

    def grads_at(which, at=None):
        down = which // fit * length
        if at is None:
            at = pl.ds(down, length)
        else:
            at = pl.ds(pl.multiple_of(at + down, block), block)
        return s.outer_w.at[at, which % fit * own_width : (which % fit + 1) * own_width]

    def settle(b, carry):
        at = nr_rows(b)
        for which in range(3):
            target = grads_at(which, b * block)
            if which == 0:
                target[...] = (s.mixed[:, at].T * scale).astype(half)
                continue
            for p in range(pairs):
                lane = slice(p * 128, (p + 1) * 128)
                if which == 1:
                    target[:, lane] = (key_block(p, b)[...] * scale).astype(half)
                else:
                    target[:, lane] = value_block(p, b)[...].astype(half)
        return carry

    lax.fori_loop(0, size.seq, settle, 0)
    ticks(Site.settle)

    def normed_grad(owner):
        return (
            dot_nt(grads_at(0, owner * block)[...], s.query_w[...])
            + dot_nt(grads_at(1, owner * block)[...], s.key_w[...])
            + dot_nt(grads_at(2, owner * block)[...], s.value_w[...])
        )

    def held(first, owner_level):
        across_at = (first + owner_level // rows) * width
        return s.activated.at[
            row_span(owner_level % rows), pl.ds(pl.multiple_of(across_at, width), width)
        ]

    held_parts = -(-depth // rows)

    def pair_copy(owner_level):
        return remote(
            held(0, owner_level), s.pair_in.at[row_span(owner_level), :],
            s.pair_sent.at[owner_level], s.pair_got.at[owner_level],
            (place.batch, level * 2 + 1 - core),
        )

    def back_copy(owner_level, source_level):
        row, part = source_level // chips, source_level % chips
        return remote(
            held(held_parts, owner_level),
            s.back.at[part, row_span(row), :],
            s.back_sent.at[owner_level], s.back_got.at[source_level],
            (place.batch, owner_level * 2 + core),
        )

    for k in range(depth):
        owner_level = (level + 1 + k) % depth
        held(0, owner_level)[...] = normed_grad(owner_level * 2 + 1 - core).astype(half)
        pair_copy(owner_level).start()
        ticks(Site.pair)
    for k in range(depth):
        owner_level = (level + 1 + k) % depth
        grad = normed_grad(owner_level * 2 + core)
        pair_copy(owner_level).wait_recv()
        grad = grad + s.pair_in[row_span(owner_level), :].astype(full)
        held(held_parts, owner_level)[...] = grad.astype(half)
        if k < depth - 1:
            back_copy(owner_level, level).start()
        else:
            back_own = pltpu.make_async_copy(
                held(held_parts, level),
                s.back.at[level % chips, row_span(level // chips), :],
                s.own_sem.at[4],
            )
            back_own.start()
        ticks(Site.give)

    for which, name in enumerate((Product.query, Product.key, Product.value)):
        value = dot_tn(nr[...], grads_at(which)[...])
        base = products.index((name, 0)) * product_rows
        for c in range(own_width // 128):
            at = pl.multiple_of(base + (my_group * (own_width // 128) + c) * width, width)
            s.mine[pl.ds(at, width), :] = value[:, c * 128 : (c + 1) * 128].astype(half)
        ticks(Site.weights)

    ticks(Site.rows)
    back_own.wait()
    for k in range(1, depth):
        source_level = (level + k) % depth
        back_copy(source_level, source_level).wait_recv()

    def first_norm(r, carry):
        at = row_span(r)
        grad = s.back[0, at, :].astype(full)
        for part in range(1, chips):
            grad = grad + s.back[part, at, :].astype(full)
        scaled, inverse = centred_rows(s.pooled[at, :])
        low = s.grad_resid[at, :] + norm_back(grad, scaled, inverse, gain_one[...])
        low = low.astype(half)
        s.normed[at, :] = low
        for k in range(3):
            put_third(6 + k, dot_nt(low, s.pool_w[k * width : (k + 1) * width, :]))
        for c in range(lanes):
            lane = slice(c * 128, (c + 1) * 128)
            s.edge_out[r, :, lane] = stage[c, 0:8, :]
            s.edge_end[r, :, lane] = stage[c, 3 * block - 8 : 3 * block + 8, :]
            s.raised[r, :, lane] = stage[c, 8 : 8 + 3 * block, :].astype(half)
        return (
            carry[0] + jnp.sum(grad * scaled, axis=0, keepdims=True),
            carry[1] + jnp.sum(grad, axis=0, keepdims=True),
            carry[2] + jnp.sum(low.astype(full), axis=0, keepdims=True),
        )

    output_copy.wait()
    for k in range(1, depth):
        row_from((level + k) % depth).wait_send()
    nothing = jnp.zeros((1, width), full)
    totals = (nothing,) * 3
    for r in range(rows):
        totals = first_norm(r, totals)
        ticks(Site.norm_one)
    put_small(Small.gain_one, 0, totals[0])
    put_small(Small.shift_one, 0, totals[1])
    put_small(Small.pool_bias, 0, totals[2])
    edge_copy = remote(
        s.edge_out, s.edge_in, s.rim_sem.at[2], s.rim_sem.at[3],
        (place.batch, (me + size.seq - 1) % size.seq),
    )

    @pl.when(me > 0)
    def _():
        edge_copy.start()

    small = SumSmall(place, small_block, s.small_landing,
                     [s.small_sem.at[0], s.small_sem.at[1]])
    small.send(0)
    for k in range(3):
        at = slice(k * width, (k + 1) * width)
        put_product(tile_at(Product.pool, k, 0), dot_tn(s.groups[:, at], s.normed[...]))
        ticks(Site.pool)

    @pl.when(me < size.seq - 1)
    def _():
        edge_copy.wait_recv()

    edge_row = lax.broadcasted_iota(jnp.int32, (16, width), 0)
    for r in range(rows):
        edge = jnp.where(me < size.seq - 1, s.edge_in[r], 0.0)
        edge = jnp.concatenate([edge, edge], axis=0)
        edge = jnp.where(edge_row >= 14, edge, s.edge_end[r])
        s.raised[r, 3 * block - 16 : 3 * block, :] = edge.astype(half)
    shift_copy = pltpu.make_async_copy(s.raised, shift_hbm, s.own_sem.at[5])
    shift_copy.start()

    rest = [chunk_of[name] for name in finish_order if name in chunk_of]
    small_stage, last_stage = 0, len(place.sizes)
    for number, c in enumerate(rest):
        if reached[c] < big.events:
            sum_step(c)
        if number % 4 == 3 and small_stage < last_stage:
            small.receive(small_stage)
            small_stage += 1
            if small_stage < last_stage:
                small.send(small_stage)
    while small_stage < last_stage:
        small.receive(small_stage)
        small_stage += 1
        if small_stage < last_stage:
            small.send(small_stage)
    for c in range(len(chunks)):
        while reached[c] < big.events:
            sum_step(c)
    small_out[...] = small_block[last_stage]

    shift_copy.wait()

    @pl.when(me < size.seq - 1)
    def _():
        rim_copy.wait_send()

    @pl.when(me > 0)
    def _():
        edge_copy.wait_send()

    for k in range(1, depth):
        other = (level + k) % depth
        back_copy(other, other).wait_send()
    for k in range(depth):
        across(k, core).wait_send()
        pair_copy(k).wait_send()
    for k in range(1, size.seq):
        other = (me + k) % size.seq
        att_copy(other, other // per_row, other % per_row, other).wait_send()
        grad_copy(other, other).wait_send()
    big.finish()
    small.finish()


def scratch_plan(size, chunks):
    tokens, length, width, hidden = size.tokens, size.length, size.width, size.hidden
    rows, block, depth = size.rows, size.block, size.depth
    own, pairs, heads = size.own_width, size.pairs, size.own_heads
    near = size.reach + 1
    stages = stage_sizes(size.batch, size.seq)
    orders = axis_orders(size, len(chunks))
    slots = sum_slots(size.batch, size.seq)
    dma = pltpu.SemaphoreType.DMA
    total = sum(chunks)
    return dict(
        x=pltpu.VMEM((2, 3 * block, width), half),
        raised=pltpu.VMEM((rows, 3 * block, width), half),
        pool_w=pltpu.VMEM((3 * width, width), half),
        up_w=pltpu.VMEM((width, 3 * width), half),
        query_w=pltpu.VMEM((width, own), half),
        key_w=pltpu.VMEM((width, own), half),
        value_w=pltpu.VMEM((width, own), half),
        outer_w=pltpu.VMEM((hidden, width), half),
        inner_w=pltpu.VMEM((width, hidden), half),
        out_w=pltpu.VMEM((width, width), half),
        rim=pltpu.VMEM((rows, 16, width), half),
        stage=pltpu.VMEM((size.lanes, 3 * block + 8, 128), full),
        groups=pltpu.VMEM((tokens, 3 * width), half),
        dy=pltpu.VMEM((tokens, 3 * width), half),
        grad_resid=pltpu.VMEM((tokens, width), full),
        grad_branch=pltpu.VMEM((tokens, width), half),
        pooled=pltpu.VMEM((tokens, width), full),
        normed=pltpu.VMEM((tokens, width), half),
        nr=pltpu.VMEM((length, width), half),
        grad_inner=pltpu.VMEM((tokens, hidden), half),
        activated=pltpu.VMEM((tokens, hidden), half),
        qt=pltpu.VMEM((heads, 128, length), half),
        kt=pltpu.VMEM((heads, 80, length), half),
        vt=pltpu.VMEM((own, length), half),
        k=pltpu.VMEM((pairs, length, 128), half),
        v=pltpu.VMEM((pairs, length, 128), half),
        work=pltpu.VMEM((2 * near, size.span, size.span), full),
        expo=pltpu.VMEM((heads, len(size.tiles), size.span, size.span), half),
        inverse=pltpu.VMEM((heads, 8, length), full),
        mixed=pltpu.VMEM((own, length), full),
        att_out=pltpu.VMEM((length, own), half),
        att=pltpu.VMEM((tokens, width), half),
        residual=pltpu.VMEM((tokens, width), full),
        normed_two=pltpu.VMEM((tokens, width), half),
        grad_att=pltpu.VMEM((tokens, width), half),
        grad_heads=pltpu.VMEM((length, own), half),
        slope_sum=pltpu.VMEM((heads, 8, size.span), full),
        pair_in=pltpu.VMEM((depth * block, width), half),
        back=pltpu.VMEM((size.chips_per_row, tokens, width), half),
        edge_out=pltpu.VMEM((rows, 8, width), full),
        edge_in=pltpu.VMEM((rows, 8, width), full),
        edge_end=pltpu.VMEM((rows, 16, width), full),
        mine=pltpu.VMEM((total, 128), half),
        landing=pltpu.VMEM((SumPieces.landing_rows(size.batch, size.seq, chunks, orders), 128), half),
        piece=pltpu.VMEM((total // (size.batch * size.seq), 128), half),
        small_block=pltpu.VMEM((len(stages) + 1, small_rows, 128), full),
        small_landing=pltpu.VMEM((sum(stages), small_rows, 128), full),
        load_sem=dma((10,)),
        x_sem=dma((2,)),
        rim_sem=dma((4,)),
        own_sem=dma((6,)),
        row_sent=dma((depth,)),
        row_got=dma((depth,)),
        across_sent=dma((depth,)),
        across_got=dma((depth,)),
        att_sent=dma((size.seq,)),
        att_got=dma((size.seq,)),
        grad_sent=dma((size.seq,)),
        grad_got=dma((size.seq,)),
        pair_sent=dma((depth,)),
        pair_got=dma((depth,)),
        back_sent=dma((depth,)),
        back_got=dma((depth,)),
        sum_sem=dma((4, len(chunks), slots)),
        keep_sem=dma((len(chunks),)),
        small_sem=dma((2, slots)),
    )


def widen_kernel(plan, steps, places, sums, shift, cotangent, small, *refs):
    outs = dict(zip(plan, refs[: len(plan)]))
    grad_inputs = refs[len(plan)]
    vectors = refs[len(plan) + 1 : len(plan) + 1 + len(places)]
    source, target, moved, kept, result, load_sem, store_sem, row_sem = refs[
        len(plan) + 1 + len(places) :
    ]
    rows = shift.shape[0]
    deep = source.shape[0]
    product_rows = source.shape[1]
    width = target.shape[1]

    def load(i):
        return pltpu.make_async_copy(
            sums.at[pl.ds(i * product_rows, product_rows), :], source.at[i % deep],
            load_sem.at[i % deep],
        )

    def store(i):
        name, part = steps[i]
        out = outs[name]
        if out.shape[0] > width:
            out = out.at[pl.ds(part * width, width), :]
        elif out.shape[1] > width:
            out = out.at[:, pl.ds(part * width, width)]
        return pltpu.make_async_copy(target.at[i % deep], out, store_sem.at[i % deep])

    def row_loads(r):
        return (
            pltpu.make_async_copy(shift.at[r], moved.at[r % 2], row_sem.at[0, r % 2]),
            pltpu.make_async_copy(cotangent.at[r], kept.at[r % 2], row_sem.at[1, r % 2]),
        )

    def row_store(r):
        return pltpu.make_async_copy(result.at[r % 2], grad_inputs.at[r], row_sem.at[2, r % 2])

    for i in range(deep - 1):
        load(i).start()
    for at, out in zip(places, vectors):
        count = out.shape[-1]
        for c in range(0, count, 128):
            part = min(128, count - c)
            if len(out.shape) == 1:
                out[c : c + part] = small[at + c // 128, :part]
            else:
                out[:, c : c + part] = small[at + c // 128 : at + c // 128 + 1, :part]
    for copy in row_loads(0):
        copy.start()
    for r in range(rows):
        if r + 1 < rows:
            for copy in row_loads(r + 1):
                copy.start()
        for copy in row_loads(r):
            copy.wait()
        if r >= 2:
            row_store(r - 2).wait()

        def add_rows(b, carry):
            at = pl.ds(pl.multiple_of(b * 64, 64), 64)
            result[r % 2, at, :] = moved[r % 2, at, :].astype(full) + kept[
                r % 2, at, :
            ].astype(full)
            return carry

        lax.fori_loop(0, result.shape[1] // 64, add_rows, 0)
        row_store(r).start()
    for i in range(len(steps)):
        if i + deep - 1 < len(steps):
            load(i + deep - 1).start()
        load(i).wait()
        if i >= deep:
            store(i - deep).wait()

        def convert(b, carry):
            at = pl.multiple_of(b * 64, 64)
            for c in range(product_rows // width):
                target[i % deep, pl.ds(at, 64), c * 128 : (c + 1) * 128] = source[
                    i % deep, pl.ds(c * width + at, 64), :
                ].astype(full)
            return carry

        lax.fori_loop(0, width // 64, convert, 0)
        store(i).start()
    for r in range(max(0, rows - 2), rows):
        row_store(r).wait()
    for i in range(max(0, len(steps) - deep), len(steps)):
        store(i).wait()


def widen(sums, shift, cotangent, small, counts, shapes, steps):
    any_space = pl.BlockSpec(memory_space=pl.ANY)
    names = tuple(shapes)
    width = shift.shape[2]
    deep = 6
    outs = [jax.ShapeDtypeStruct(shapes[name], full) for name in names]
    outs.append(jax.ShapeDtypeStruct(shift.shape, full))
    outs += [
        jax.ShapeDtypeStruct(
            (count,) if count % 1024 == 512 and count > 512 else (1, count), full
        )
        for count in counts.values()
    ]
    vmem = pl.BlockSpec(memory_space=pltpu.VMEM)
    row = shift.shape[1:]
    product_rows = sums.shape[0] // len(steps)
    results = pl.pallas_call(
        functools.partial(widen_kernel, names, steps, tuple(counts)),
        out_shape=outs,
        in_specs=[any_space] * 3 + [vmem],
        out_specs=[any_space] * (len(names) + 1) + [vmem] * len(counts),
        scratch_shapes=[
            pltpu.VMEM((deep, product_rows, 128), half),
            pltpu.VMEM((deep, width, width), full),
            pltpu.VMEM((2,) + row, half),
            pltpu.VMEM((2,) + row, half),
            pltpu.VMEM((2,) + row, full),
            pltpu.SemaphoreType.DMA((deep,)),
            pltpu.SemaphoreType.DMA((deep,)),
            pltpu.SemaphoreType.DMA((3, 2)),
        ],
        name="widen",
    )(sums, shift, cotangent, small)
    vectors = {
        at: value.reshape(-1) for at, value in zip(counts, results[len(names) + 1 :])
    }
    return dict(zip(names, results)), results[len(names)], vectors


def local(
    inputs,
    cotangent,
    doc_lengths,
    pool_weight,
    pool_bias,
    gain_one,
    shift_one,
    query_weight,
    key_weight,
    value_weight,
    out_weight,
    slopes,
    gain_two,
    shift_two,
    inner_weight,
    inner_bias,
    outer_weight,
    outer_bias,
    up_weight,
    up_bias,
):
    rows, block_len, width = inputs.shape
    hidden = inner_weight.shape[1]
    size = Sizes(
        lax.axis_size("batch"), lax.axis_size("seq"), rows, block_len // 3, width,
        hidden, slopes.shape[0],
    )
    steps = product_list(size.parts)
    product_rows = width * size.lanes
    chunks = [2 * product_rows] * (len(steps) // 2)
    if product_rows % (16 * size.batch * size.seq) == 0:
        chunks[-1:] = [product_rows] * 2
    total = len(steps) * product_rows
    vmem = pl.BlockSpec(memory_space=pltpu.VMEM)
    smem = pl.BlockSpec(memory_space=pltpu.SMEM)
    any_space = pl.BlockSpec(memory_space=pl.ANY)
    plan = scratch_plan(size, chunks)
    vectors = (
        pool_bias, gain_one, shift_one, gain_two, shift_two, inner_bias, outer_bias, up_bias,
    )
    output, shift, sums, small = pl.pallas_call(
        functools.partial(layer_kernel, size, chunks),
        out_shape=(
            jax.ShapeDtypeStruct(inputs.shape, half),
            jax.ShapeDtypeStruct(inputs.shape, half),
            jax.ShapeDtypeStruct((total, 128), half),
            jax.ShapeDtypeStruct((small_rows, 128), full),
        ),
        in_specs=[smem, smem] + [vmem] * 8 + [any_space] * 10,
        out_specs=(any_space, any_space, any_space, vmem),
        scratch_shapes=list(plan.values()),
        compiler_params=pltpu.CompilerParams(
            collective_id=0, has_side_effects=True, vmem_limit_bytes=67043328
        ),
        name="layer",
    )(
        doc_lengths, slopes, *(v.reshape(1, -1) for v in vectors[:-1]), up_bias,
        inputs, cotangent, pool_weight, query_weight, key_weight, value_weight,
        out_weight, inner_weight, outer_weight, up_weight,
    )
    shapes = {
        Product.inner: inner_weight.shape, Product.outer: outer_weight.shape, Product.up: up_weight.shape,
        Product.out: out_weight.shape, Product.query: query_weight.shape, Product.key: key_weight.shape,
        Product.value: value_weight.shape, Product.pool: pool_weight.shape,
    }
    counts = {
        Small.pool_bias: width, Small.gain_one: width, Small.shift_one: width,
        Small.slopes: slopes.shape[0], Small.gain_two: width, Small.shift_two: width,
        Small.inner_bias: hidden, Small.outer_bias: width, Small.up_bias: 3 * width,
    }
    grads, input_grad, vector = widen(sums, shift, cotangent, small, counts, shapes, steps)

    return (
        output,
        input_grad,
        grads[Product.pool],
        vector[Small.pool_bias],
        vector[Small.gain_one],
        vector[Small.shift_one],
        grads[Product.query],
        grads[Product.key],
        grads[Product.value],
        grads[Product.out],
        vector[Small.slopes],
        vector[Small.gain_two],
        vector[Small.shift_two],
        grads[Product.inner],
        vector[Small.inner_bias],
        grads[Product.outer],
        vector[Small.outer_bias],
        grads[Product.up],
        vector[Small.up_bias],
    )


def solution(mesh):
    blocks = P("batch", "seq", None)
    in_specs = (blocks, blocks, P("batch", None)) + (P(),) * 17
    out_specs = (blocks, blocks) + (P(),) * 17
    return jax.shard_map(local, mesh=mesh, in_specs=in_specs, out_specs=out_specs, check_vma=False)
```

time: 197 us -> 173 us (0.88)
  Pallas kernels: 190 us -> 171 us
  local copies, waits for them, and re-layouts: 4.76 us -> 1.15 us
    pallas_call x2, Pallas kernels: 190 us -> 171 us  [the longest x1 156 us: local(): pl.pallas_call(functools.partial(layer_kernel, size, chunks), out_shape=(...]
    reshape x4 -> x0, local copies, waits for them, and re-layouts: 3.1 us -> none  [the longest x3 1.8 us: vector(): return small[at:at + count // 128].reshape(count)]
where the time goes in v3:
time: 173 us
  Pallas kernels  171 us (99%)
    pallas_call x1, Pallas kernels, local(): pl.pallas_call(functools.partial(layer_kernel, size, chunks), out_shape=(...  156 us
    pallas_call x1, Pallas kernels, widen(): pl.pallas_call(functools.partial(widen_kernel, names, steps, tuple(counts...  14.3 us

profile of v3, /device:TPU:0, one launch (start us, length us, event | category | flops | bytes accessed | tf_op | source)
XLA Modules:
  0.0 172.5 jit_solution(16085103091450754351)
XLA Ops:
  0.7 156.4 %layer.1 = (bf16[4,384,512]{2,1,0:T(8,128)(2,1)}, bf16[4,384,512]{2,1,0:T(8,128)(2,1)}, bf16[36864,128]{1,0:T(8,128)(2,1)}, f32[56,128]{1,0:T(8,128)}) custom-call(s32[4,8]{1,0:T(4,128)} %docs.1, f32[8]{0:T(128)} %slopes.1, f32[1,512]{1,0:T(1,128)} %bitcast.16, f32[1,512]{1,0:T(1,128)} %bitcast.17, f32[1,512]{1,0:T(1,128)} %bitcast.18, f32[1,512]{1,0:T(1,128)} %bitcast.19, ...), custom_call_target="tpu_custom_call" | custom-call | tf_op jit(solution)/shard_map/layer/pallas_call | solution.py:1387
  157.0 0.0 copy-start
  157.1 14.3 %widen.1 = (f32[512,2048]{1,0:T(8,128)}, f32[2048,512]{1,0:T(8,128)}, f32[512,1536]{1,0:T(8,128)}, f32[512,512]{1,0:T(8,128)}, f32[512,512]{1,0:T(8,128)}, /*ind...) custom-call(bf16[36864,128]{1,0:T(8,128)(2,1)} %get-tuple-element.42, ...), custom_call_target="tpu_custom_call" | custom-call | tf_op jit(solution)/shard_map/widen/pallas_call | solution.py:1323
  171.3 0.0 copy-done
  171.4 1.1 copy.40
Async XLA Ops:
  157.0 14.3 %copy-start = (bf16[4,384,512]{2,1,0:T(8,128)(2,1)S(1)}, bf16[4,384,512]{2,1,0:T(8,128)(2,1)}, u32[]{:S(2)}) copy-start(bf16[4,384,512]{2,1,0:T(8,128)(2,1)} %get-tuple-element.82) | copy-start | bytes 4718596

commit v4 on v3

--- a/solution.py
+++ b/solution.py
@@ -401,54 +401,44 @@
     def tile_at(name, part, lane):
         return products.index((name, part)) * product_rows + lane * width
 
-    loads = SimpleNamespace()
-
-    def load(source, target):
-        copy = pltpu.make_async_copy(source, target, s.load_sem.at[len(vars(loads))])
-        copy.start()
-        return copy
-
-    first_column = pl.multiple_of(my_group * own_width, own_width)
-
-    def x_load(step):
-        return pltpu.make_async_copy(
-            inputs_hbm.at[(my_row + 1 + step) % rows], s.x.at[step % 2],
-            s.x_sem.at[step % 2],
-        )
-
-    x_load(0).start()
-    loads.pool = load(pool_hbm, s.pool_w)
-    loads.dy = load(cotangent_hbm, s.raised)
-    loads.up = load(up_hbm, s.up_w)
-    loads.query = load(query_hbm.at[:, pl.ds(first_column, own_width)], s.query_w)
-    loads.key = load(key_hbm.at[:, pl.ds(first_column, own_width)], s.key_w)
-    loads.value = load(value_hbm.at[:, pl.ds(first_column, own_width)], s.value_w)
-    loads.outer = load(outer_hbm, s.outer_w)
-    loads.out = load(out_hbm, s.out_w)
-    loads.inner = load(inner_hbm, s.inner_w)
-
     barrier = pltpu.get_barrier_semaphore()
     greeted = [(place.batch, (me + k) % size.seq) for k in range(1, size.seq)]
     for stage in (1, 2):
         greeted += [place.partner(stage, k) for k in range(1, place.sizes[stage])]
     for device in greeted:
         pl.semaphore_signal(barrier, inc=1, device_id=device, device_id_type=MESH)
-    pl.semaphore_wait(barrier, len(greeted))
+
+    loads = SimpleNamespace()
+
+    def load(source, target):
+        copy = pltpu.make_async_copy(source, target, s.load_sem.at[len(vars(loads))])
+        copy.start()
+        return copy
+
+    first_column = pl.multiple_of(my_group * own_width, own_width)
+
+    def x_load(step):
+        return pltpu.make_async_copy(
+            inputs_hbm.at[(my_row + 1 + step) % rows], s.x.at[step % 2],
+            s.x_sem.at[step % 2],
+        )
+
+    x_load(0).start()
+    loads.dy = load(cotangent_hbm, s.raised)
+    loads.up = load(up_hbm, s.up_w)
+    loads.pool = load(pool_hbm, s.pool_w)
+    loads.outer = load(outer_hbm, s.outer_w)
+    loads.query = load(query_hbm.at[:, pl.ds(first_column, own_width)], s.query_w)
+    loads.key = load(key_hbm.at[:, pl.ds(first_column, own_width)], s.key_w)
+    loads.value = load(value_hbm.at[:, pl.ds(first_column, own_width)], s.value_w)
+    loads.out = load(out_hbm, s.out_w)
+    loads.inner = load(inner_hbm, s.inner_w)
 
     def remote(source, target, sent, got, device):
         return pltpu.make_async_remote_copy(
             src_ref=source, dst_ref=target, send_sem=sent, recv_sem=got,
             device_id=device, device_id_type=MESH,
         )
-
-    rim_copy = remote(
-        inputs_hbm.at[:, pl.ds(3 * block - 16, 16), :], s.rim,
-        s.rim_sem.at[0], s.rim_sem.at[1], (place.batch, (me + 1) % size.seq),
-    )
-
-    @pl.when(me < size.seq - 1)
-    def _():
-        rim_copy.start()
 
     small_block = s.small_block
     small_block[0] = jnp.zeros((small_rows, 128), full)
@@ -502,6 +492,26 @@
     for k in range(3):
         put_small(Small.up_bias, k * width, sums[k])
     put_small(Small.outer_bias, 0, sums[3])
+
+    pl.semaphore_wait(barrier, len(greeted))
+    rim_copy = remote(
+        inputs_hbm.at[:, pl.ds(3 * block - 16, 16), :], s.rim,
+        s.rim_sem.at[0], s.rim_sem.at[1], (place.batch, (me + 1) % size.seq),
+    )
+
+    @pl.when(me < size.seq - 1)
+    def _():
+        rim_copy.start()
+
+    loads.outer.wait()
+
+    def before_activation(j, carry):
+        at = pl.ds(pl.multiple_of(j * width, width), width)
+        grad = dot_nt(s.grad_branch[...], s.outer_w[at, :])
+        s.grad_inner[:, at] = grad.astype(half)
+        return carry
+
+    lax.fori_loop(0, parts, before_activation, 0)
 
     @pl.when(me > 0)
     def _():
@@ -555,16 +565,6 @@
             )
             own_copy.start()
 
-    loads.outer.wait()
-
-    def before_activation(j, carry):
-        at = pl.ds(pl.multiple_of(j * width, width), width)
-        grad = dot_nt(s.grad_branch[...], s.outer_w[at, :])
-        s.grad_inner[:, at] = grad.astype(half)
-        return carry
-
-    lax.fori_loop(0, parts, before_activation, 0)
-
     def across(source_level, owner_core):
         owner = source_level * 2 + owner_core
         return remote(
@@ -645,7 +645,11 @@
     def head_slope(h):
         return slopes[my_group * size.own_heads + h]
 
-    for i in range(size.query_blocks):
+    turns = [
+        t // 2 if t % 2 == 0 else size.query_blocks - 1 - t // 2
+        for t in range(size.query_blocks)
+    ]
+    for i in turns:
         cols = slice(i * span, (i + 1) * span)
         place_q = 3 * (i * span + lax.broadcasted_iota(jnp.int32, (1, span), 1))
         start = jnp.zeros((1, span), jnp.int32)

time: 173 us -> 172 us (level)
  no operation moved by 1% of the time
where the time goes in v4:
time: 172 us
  Pallas kernels  170 us (99%)
    pallas_call x1, Pallas kernels, local(): pl.pallas_call(functools.partial(layer_kernel, size, chunks), out_shape=(...  156 us
    pallas_call x1, Pallas kernels, widen(): pl.pallas_call(functools.partial(widen_kernel, names, steps, tuple(counts...  14.3 us

profile of v4, /device:TPU:0, one launch (start us, length us, event | category | flops | bytes accessed | tf_op | source)
XLA Modules:
  0.0 171.8 jit_solution(7153353085448742748)
XLA Ops:
  0.7 155.7 %layer.1 = (bf16[4,384,512]{2,1,0:T(8,128)(2,1)}, bf16[4,384,512]{2,1,0:T(8,128)(2,1)}, bf16[36864,128]{1,0:T(8,128)(2,1)}, f32[56,128]{1,0:T(8,128)}) custom-call(s32[4,8]{1,0:T(4,128)} %docs.1, f32[8]{0:T(128)} %slopes.1, f32[1,512]{1,0:T(1,128)} %bitcast.16, f32[1,512]{1,0:T(1,128)} %bitcast.17, f32[1,512]{1,0:T(1,128)} %bitcast.18, f32[1,512]{1,0:T(1,128)} %bitcast.19, ...), custom_call_target="tpu_custom_call" | custom-call | tf_op jit(solution)/shard_map/layer/pallas_call | solution.py:1391
  156.3 0.0 copy-start
  156.3 14.3 %widen.1 = (f32[512,2048]{1,0:T(8,128)}, f32[2048,512]{1,0:T(8,128)}, f32[512,1536]{1,0:T(8,128)}, f32[512,512]{1,0:T(8,128)}, f32[512,512]{1,0:T(8,128)}, /*ind...) custom-call(bf16[36864,128]{1,0:T(8,128)(2,1)} %get-tuple-element.42, ...), custom_call_target="tpu_custom_call" | custom-call | tf_op jit(solution)/shard_map/widen/pallas_call | solution.py:1327
  170.6 0.0 copy-done
  170.6 1.1 copy.40
Async XLA Ops:
  156.3 14.3 %copy-start = (bf16[4,384,512]{2,1,0:T(8,128)(2,1)S(1)}, bf16[4,384,512]{2,1,0:T(8,128)(2,1)}, u32[]{:S(2)}) copy-start(bf16[4,384,512]{2,1,0:T(8,128)(2,1)} %get-tuple-element.82) | copy-start | bytes 4718596

commit v5 on v4

--- a/solution.py
+++ b/solution.py
@@ -1312,7 +1312,7 @@
     any_space = pl.BlockSpec(memory_space=pl.ANY)
     names = tuple(shapes)
     width = shift.shape[2]
-    deep = 6
+    deep = 9
     outs = [jax.ShapeDtypeStruct(shapes[name], full) for name in names]
     outs.append(jax.ShapeDtypeStruct(shift.shape, full))
     outs += [

time: 172 us -> 172 us (level)
  no operation moved by 1% of the time
where the time goes in v5:
time: 172 us; the launch traced here: 171 us
  Pallas kernels  170 us (99%)
    pallas_call x1, Pallas kernels, local(): pl.pallas_call(functools.partial(layer_kernel, size, chunks), out_shape=(...  156 us
    pallas_call x1, Pallas kernels, widen(): pl.pallas_call(functools.partial(widen_kernel, names, steps, tuple(counts...  13.9 us

profile of v5, /device:TPU:0, one launch (start us, length us, event | category | flops | bytes accessed | tf_op | source)
XLA Modules:
  0.0 171.4 jit_solution(17883889876970302354)
XLA Ops:
  0.7 155.7 %layer.1 = (bf16[4,384,512]{2,1,0:T(8,128)(2,1)}, bf16[4,384,512]{2,1,0:T(8,128)(2,1)}, bf16[36864,128]{1,0:T(8,128)(2,1)}, f32[56,128]{1,0:T(8,128)}) custom-call(s32[4,8]{1,0:T(4,128)} %docs.1, f32[8]{0:T(128)} %slopes.1, f32[1,512]{1,0:T(1,128)} %bitcast.16, f32[1,512]{1,0:T(1,128)} %bitcast.17, f32[1,512]{1,0:T(1,128)} %bitcast.18, f32[1,512]{1,0:T(1,128)} %bitcast.19, ...), custom_call_target="tpu_custom_call" | custom-call | tf_op jit(solution)/shard_map/layer/pallas_call | solution.py:1391
  156.3 0.0 copy-start
  156.3 13.9 %widen.1 = (f32[512,2048]{1,0:T(8,128)}, f32[2048,512]{1,0:T(8,128)}, f32[512,1536]{1,0:T(8,128)}, f32[512,512]{1,0:T(8,128)}, f32[512,512]{1,0:T(8,128)}, /*ind...) custom-call(bf16[36864,128]{1,0:T(8,128)(2,1)} %get-tuple-element.42, ...), custom_call_target="tpu_custom_call" | custom-call | tf_op jit(solution)/shard_map/widen/pallas_call | solution.py:1327
  170.2 0.0 copy-done
  170.3 1.1 copy.40
Async XLA Ops:
  156.3 13.9 %copy-start = (bf16[4,384,512]{2,1,0:T(8,128)(2,1)S(1)}, bf16[4,384,512]{2,1,0:T(8,128)(2,1)}, u32[]{:S(2)}) copy-start(bf16[4,384,512]{2,1,0:T(8,128)(2,1)} %get-tuple-element.82) | copy-start | bytes 4718596
